TPU v7x, 8 devices: a whole 2x2x1 slice. The times are simulated.
8 devices in a mesh: dp: 1 (over z), ctx: 8 (over y, x, core).
Axes of the slice: x: 2, y: 2, z: 1, core: 2. Of those that a mesh axis runs over, the one named last changes fastest.
Arguments:
- x_seq: bfloat16 [512, 2560], P(('dp', 'ctx'))
- pos_ids: int32 [512], P(('dp', 'ctx'))
- seg_ids: int32 [512], P(('dp', 'ctx'))
- w_dq: bfloat16 [2560, 768], replicated
- w_uq: bfloat16 [768, 2560], replicated
- w_qr: bfloat16 [768, 1280], replicated
- w_dkv: bfloat16 [2560, 256], replicated
- w_kr: bfloat16 [2560, 32], replicated
- w_uk: bfloat16 [256, 2560], replicated
- w_uv: bfloat16 [256, 2560], replicated
- w_out: bfloat16 [2560, 2560], replicated
- gain_q: bfloat16 [768], replicated
- gain_kv: bfloat16 [256], replicated
Outputs:
- output: bfloat16 [512, 2560], P(('dp', 'ctx'))
All inputs are finite; a program needn't handle non-finite values.
Results may differ from a plain program's by a relative error of at most 0.0079002.
Values are sent between devices in bfloat16 or wider.
A program may use at most 1 GiB of HBM per device.

v0:
```python
import jax
import jax.numpy as jnp
from jax import lax
from jax.sharding import PartitionSpec as P, NamedSharding

NORM_EPS = 1e-6


def rms_norm(vals, gain):
    mean_sq = jnp.mean(vals * vals, axis=-1, keepdims=True)
    return (vals * lax.rsqrt(mean_sq + NORM_EPS) * gain.astype(jnp.float32)).astype(jnp.bfloat16)


def rope_tables(pos_ids, rope_dim):
    half_dim = rope_dim // 2
    inv_freq = 10000.0 ** (-2.0 * jnp.arange(half_dim, dtype=jnp.float32) / rope_dim)
    angles = pos_ids.astype(jnp.float32)[:, None] * inv_freq[None, :]
    return jnp.cos(angles), jnp.sin(angles)


def apply_rope(vals, cos_tab, sin_tab):
    half_dim = vals.shape[-1] // 2
    lead_half = vals[..., :half_dim]
    tail_half = vals[..., half_dim:]
    return jnp.concatenate([lead_half * cos_tab - tail_half * sin_tab, tail_half * cos_tab + lead_half * sin_tab], axis=-1)


def solution(mesh):
    group_size = mesh.shape['ctx']
    shift_pairs = [(source, (source + 1) % group_size) for source in range(group_size)]
    row_spec = P(('dp', 'ctx'), None)
    id_spec = P(('dp', 'ctx'))

    def per_device(x_rows, pos_rows, seg_rows, w_dq, w_uq, w_qr, w_dkv, w_kr, w_uk, w_uv, w_out, gain_q, gain_kv):
        seq_dev = x_rows.shape[0]
        kv_rank = w_dkv.shape[1]
        rope_dim = w_kr.shape[1]
        num_heads = w_qr.shape[1] // rope_dim
        nope_dim = w_uq.shape[1] // num_heads
        v_dim = w_uv.shape[1] // num_heads
        score_scale = (nope_dim + rope_dim) ** -0.5
        cos_tab, sin_tab = rope_tables(pos_rows, rope_dim)
        c_q = rms_norm(jnp.dot(x_rows, w_dq, preferred_element_type=jnp.float32), gain_q)
        q_nope = jnp.dot(c_q, w_uq, preferred_element_type=jnp.float32).astype(jnp.bfloat16).reshape(seq_dev, num_heads, nope_dim)
        q_rope = jnp.dot(c_q, w_qr, preferred_element_type=jnp.float32).reshape(seq_dev, num_heads, rope_dim)
        q_rope = apply_rope(q_rope, cos_tab[:, None, :], sin_tab[:, None, :]).astype(jnp.bfloat16)
        c_kv = rms_norm(jnp.dot(x_rows, w_dkv, preferred_element_type=jnp.float32), gain_kv)
        k_rope = apply_rope(jnp.dot(x_rows, w_kr, preferred_element_type=jnp.float32), cos_tab, sin_tab).astype(jnp.bfloat16)
        latents = jnp.concatenate([c_kv, k_rope], axis=1)
        key_ids = jnp.stack([pos_rows, seg_rows])
        w_uk3 = w_uk.reshape(kv_rank, num_heads, nope_dim)
        w_uv3 = w_uv.reshape(kv_rank, num_heads, v_dim)

        def attend_block(soft_state, lat_blk, ids_blk):
            run_max, run_sum, run_acc = soft_state
            c_blk = lat_blk[:, :kv_rank]
            k_nope = jnp.einsum('kc,chd->khd', c_blk, w_uk3, preferred_element_type=jnp.float32).astype(jnp.bfloat16)
            v_blk = jnp.einsum('kc,chd->khd', c_blk, w_uv3, preferred_element_type=jnp.float32).astype(jnp.bfloat16)
            scores = jnp.einsum('qhd,khd->qhk', q_nope, k_nope, preferred_element_type=jnp.float32)
            scores = (scores + jnp.einsum('qhr,kr->qhk', q_rope, lat_blk[:, kv_rank:], preferred_element_type=jnp.float32)) * score_scale
            allowed = ((ids_blk[0][None, :] <= pos_rows[:, None]) & (ids_blk[1][None, :] == seg_rows[:, None]))[:, None, :]
            scores = jnp.where(allowed, scores, -1e30)
            new_max = jnp.maximum(run_max, jnp.max(scores, axis=-1))
            weights = jnp.where(allowed, jnp.exp(scores - new_max[..., None]), 0.0)
            rescale = jnp.exp(run_max - new_max)
            run_sum = run_sum * rescale + jnp.sum(weights, axis=-1)
            run_acc = run_acc * rescale[..., None] + jnp.einsum('qhk,khd->qhd', weights.astype(jnp.bfloat16), v_blk, preferred_element_type=jnp.float32)
            return new_max, run_sum, run_acc

        soft_state = (jnp.full((seq_dev, num_heads), -1e30, jnp.float32), jnp.zeros((seq_dev, num_heads), jnp.float32), jnp.zeros((seq_dev, num_heads, v_dim), jnp.float32))
        soft_state = attend_block(soft_state, latents, key_ids)

        def hop_step(hop_index, loop_carry):
            lat_blk, ids_blk, block_state = loop_carry
            lat_blk = lax.ppermute(lat_blk, 'ctx', shift_pairs)
            ids_blk = lax.ppermute(ids_blk, 'ctx', shift_pairs)
            return lat_blk, ids_blk, attend_block(block_state, lat_blk, ids_blk)

        final_carry = lax.fori_loop(1, group_size, hop_step, (latents, key_ids, soft_state))
        _, run_sum, run_acc = final_carry[2]
        attn_out = (run_acc / run_sum[..., None]).astype(jnp.bfloat16).reshape(seq_dev, num_heads * v_dim)
        return jnp.dot(attn_out, w_out, preferred_element_type=jnp.float32).astype(jnp.bfloat16)

    return jax.shard_map(per_device, mesh=mesh, in_specs=(row_spec, id_spec, id_spec) + (P(),) * 10, out_specs=row_spec, check_vma=False)
```

profile of v0, /device:TPU:0, one launch (start us, length us, event | category | flops | bytes accessed | tf_op | source)
XLA Modules:
  0.0 139.6 jit_solution(3905697729231543407)
XLA Ops:
  0.0 3.3 %multiply_reduce_fusion = (f32[64]{0:T(128)S(1)}, f32[64,768]{1,0:T(8,128)S(1)}) fusion(bf16[64,2560]{1,0:T(8,128)(2,1)} %param.15, bf16[2560,768]{1,0:T(8,128)(2,1)} %param.18), kind=kOutput, calls=%fused_computation.43 | convolution fusion | flops 251756480 | bytes 4456704 | tf_op jit(solution)/shard_map/dot_general | solution.py:43
  3.4 0.9 fusion.28
  4.6 0.8 subtract_convert_fusion
  5.5 0.9 convolution_convert_fusion.3
  6.7 2.0 %multiply_reduce_fusion.1 = (f32[64]{0:T(128)S(1)}, f32[64,256]{1,0:T(8,128)S(1)}) fusion(bf16[64,2560]{1,0:T(8,128)(2,1)S(1)} %copy-done.3, bf16[2560,256]{1,0:T(8,128)(2,1)} %param.21), kind=kOutput, calls=%fused_computation.45 | convolution fusion | flops 83918784 | bytes 1704192 | tf_op jit(solution)/shard_map/dot_general | solution.py:47
  8.8 2.4 %copy.46 = bf16[256,2560]{0,1:T(8,128)(2,1)} copy(bf16[256,2560]{1,0:T(8,128)(2,1)} %param.23) | data formatting | bytes 2621440 | tf_op args[8]
  11.3 3.5 %convolution_bitcast_fusion.3 = f32[64,40,64]{0,2,1:T(8,128)} fusion(bf16[256,40,64]{0,2,1:T(8,128)(2,1)} %bitcast.9, bf16[64,256]{1,0:T(8,128)(2,1)S(1)} %multiply_convert_fusion.1, bf16[64,40,64]{2,1,0:T(8,128)(2,1)S(1)} %reshape.189), kind=kOutput, calls=%fused_computation.27 | convolution fusion | flops 105021440 | bytes 2326528 | tf_op jit(solution)/shard_map/qhd,khd->qhk/dot_general | solution.py:59
  14.7 0.8 compare_and_fusion.1
  15.6 1.9 %fusion.31 = (f32[64,40]{0,1:T(8,128)S(1)}, f32[64,40,64]{0,2,1:T(8,128)S(1)}) fusion(f32[64,40,64]{0,2,1:T(8,128)} %convolution_bitcast_fusion.3, bf16[64,16]{0,1:T(8,128)(2,1)S(1)} %get-tuple-element.144, bf16[64,16]{0,1:T(8,128)(2,1)S(1)} %get-tuple-element.145, bf16[64,40,16]{0,2,1:T(8,128)(2,1)} %get-tuple-element.137, ...), kind=kOutput, calls=%fused_computation.69 | convolution fusion | flops 11474432 | bytes 1492992 | tf_op jit(solution)/shard_map/qhr,kr->qhk/dot_general | solution.py:60
  18.4 2.4 %copy.49 = bf16[256,2560]{0,1:T(8,128)(2,1)} copy(bf16[256,2560]{1,0:T(8,128)(2,1)} %param.24) | data formatting | bytes 2621440 | tf_op args[9]
  20.9 3.3 %fusion.11 = f32[64,40,64]{0,2,1:T(8,128)} fusion(bf16[256,40,64]{0,2,1:T(8,128)(2,1)} %bitcast.13, f32[64,40,64]{0,2,1:T(8,128)S(1)} %get-tuple-element.151, f32[64,40]{0,1:T(8,128)S(1)} %copy-done.5, f32[64,40]{0,1:T(8,128)S(1)} %broadcast_maximum_fusion, pred[64,64]{0,1:T(8,128)(4,1)S(1)} %compare_and_fusion.1, ...), kind=kOutput, calls=%fused_computation.28 | convolution fusion | flops 105676800 | bytes 2678784 | tf_op jit(solution)/shard_map/qhk,khd->qhd/dot_general | solution.py:67
  24.2 1.7 %pad_maximum_fusion = bf16[64,40,32]{0,2,1:T(8,128)(2,1)} fusion(bf16[64,40,16]{0,2,1:T(8,128)(2,1)} %get-tuple-element.137, bf16[64,40,16]{0,2,1:T(8,128)(2,1)S(1)} %get-tuple-element.136), kind=kLoop, calls=%fused_computation.39 | loop fusion | flops 327680 | bytes 327680 | tf_op jit(solution)/shard_map/concatenate | solution.py:25
  26.2 2.1 %copy.47 = bf16[64,40,64]{2,0,1:T(8,128)(2,1)} copy(bf16[64,40,64]{2,1,0:T(8,128)(2,1)} %copy-done.1) | data formatting | bytes 655360 | tf_op jit(solution)/shard_map/reshape | solution.py:44
  29.0 101.3 %while.18 = (s32[]{:T(128)}, bf16[64,288]{1,0:T(8,128)(2,1)S(1)}, s32[2,64]{1,0:T(2,128)S(1)}, f32[64,40]{0,1:T(8,128)S(1)}, f32[64,40]{0,1:T(8,128)S(1)}, /*ind...) while((s32[]{:T(128)}, bf16[64,288]{1,0:T(8,128)(2,1)S(1)}, ...), condition=%wide.region_7.8_spmd, body=%wide.region_4.7_spmd.sunk | while | flops 222512128 | bytes 8873165 | solution.py:79
  29.0 0.9 collective-permute-start.1
  29.8 2.6 %collective-permute-start = (bf16[64,288]{1,0:T(8,128)(2,1)S(1)}, bf16[64,288]{1,0:T(8,128)(2,1)S(1)}, u32[]{:S(2)}, u32[]{:S(2)}) collective-permute-start(bf16[64,288]{1,0:T(8,128)(2,1)S(1)} %get-tuple-element.251), channel_id=1, source_target_pairs={{0,1},{1,2},{2,3},{3,4},{4,5},{5,6},{6,7},{7,0}} | collective-permute-start | bytes 110600 | tf_op jit(solution)/shard_map/while/body/eval_jaxpr/ppermute | solution.py:75
  32.4 1.5 %collective-permute-done.1 = s32[2,64]{1,0:T(2,128)S(1)} collective-permute-done((s32[2,64]{1,0:T(2,128)S(1)}, s32[2,64]{1,0:T(2,128)S(1)}, u32[]{:S(2)}, u32[]{:S(2)}) %collective-permute-start.1) | collective-permute-done | bytes 544 | tf_op jit(solution)/shard_map/while/body/eval_jaxpr/ppermute | solution.py:76
  34.8 3.6 %convolution_bitcast_fusion.5 = f32[64,40,64]{0,2,1:T(8,128)} fusion(bf16[64,40,64]{2,0,1:T(8,128)(2,1)} %get-tuple-element.272, bf16[256,40,64]{0,2,1:T(8,128)(2,1)} %get-tuple-element.271, bf16[64,288]{1,0:T(8,128)(2,1)S(1)} %collective-permute-done), kind=kOutput, calls=%fused_computation.3.clone.1 | convolution fusion | flops 105021440 | bytes 2326528 | tf_op jit(solution)/shard_map/while/body/eval_jaxpr/qhd,khd->qhk/dot_general | solution.py:59
  38.4 1.8 %fusion.62 = (f32[64,40]{0,1:T(8,128)S(1)}, f32[64,40,64]{0,2,1:T(8,128)S(1)}) fusion(f32[64,40,64]{0,2,1:T(8,128)} %convolution_bitcast_fusion.5, bf16[64,40,32]{0,2,1:T(8,128)(2,1)} %get-tuple-element.273, bf16[64,288]{1,0:T(8,128)(2,1)S(1)} %collective-permute-done, pred[64,64]{0,1:T(8,128)(4,1)S(1)} %compare_and_fusion.3), kind=kOutput, calls=%fused_computation.68.clone.1 | convolution fusion | flops 11138560 | bytes 1509376 | tf_op jit(solution)/shard_map/while/body/eval_jaxpr/qhr,kr->qhk/dot_general | solution.py:60
  40.6 3.8 %fusion.64 = f32[64,40,64]{0,2,1:T(8,128)} fusion(f32[64,40,64]{0,2,1:T(8,128)} %get-tuple-element.255, bf16[256,40,64]{0,2,1:T(8,128)(2,1)} %get-tuple-element.274, f32[64,40,64]{0,2,1:T(8,128)S(1)} %get-tuple-element.234, f32[64,40]{0,1:T(8,128)S(1)} %get-tuple-element.236, f32[64,40]{0,1:T(8,128)S(1)} %max.4, ...), kind=kOutput, calls=%fused_computation.4.clone.1 | convolution fusion | flops 105840640 | bytes 4014080 | tf_op jit(solution)/shard_map/while/body/eval_jaxpr/qhk,khd->qhd/dot_general | solution.py:67
  44.4 1.5 %collective-permute-start = (bf16[64,288]{1,0:T(8,128)(2,1)S(1)}, bf16[64,288]{1,0:T(8,128)(2,1)S(1)}, u32[]{:S(2)}, u32[]{:S(2)}) collective-permute-start(bf16[64,288]{1,0:T(8,128)(2,1)S(1)} %get-tuple-element.251), channel_id=1, source_target_pairs={{0,1},{1,2},{2,3},{3,4},{4,5},{5,6},{6,7},{7,0}} | collective-permute-start | bytes 110600 | tf_op jit(solution)/shard_map/while/body/eval_jaxpr/ppermute | solution.py:75
  45.9 2.4 %collective-permute-done.1 = s32[2,64]{1,0:T(2,128)S(1)} collective-permute-done((s32[2,64]{1,0:T(2,128)S(1)}, s32[2,64]{1,0:T(2,128)S(1)}, u32[]{:S(2)}, u32[]{:S(2)}) %collective-permute-start.1) | collective-permute-done | bytes 544 | tf_op jit(solution)/shard_map/while/body/eval_jaxpr/ppermute | solution.py:76
  48.3 0.7 compare_and_fusion.3
  49.1 3.6 %convolution_bitcast_fusion.5 = f32[64,40,64]{0,2,1:T(8,128)} fusion(bf16[64,40,64]{2,0,1:T(8,128)(2,1)} %get-tuple-element.272, bf16[256,40,64]{0,2,1:T(8,128)(2,1)} %get-tuple-element.271, bf16[64,288]{1,0:T(8,128)(2,1)S(1)} %collective-permute-done), kind=kOutput, calls=%fused_computation.3.clone.1 | convolution fusion | flops 105021440 | bytes 2326528 | tf_op jit(solution)/shard_map/while/body/eval_jaxpr/qhd,khd->qhk/dot_general | solution.py:59
  52.7 1.8 %fusion.62 = (f32[64,40]{0,1:T(8,128)S(1)}, f32[64,40,64]{0,2,1:T(8,128)S(1)}) fusion(f32[64,40,64]{0,2,1:T(8,128)} %convolution_bitcast_fusion.5, bf16[64,40,32]{0,2,1:T(8,128)(2,1)} %get-tuple-element.273, bf16[64,288]{1,0:T(8,128)(2,1)S(1)} %collective-permute-done, pred[64,64]{0,1:T(8,128)(4,1)S(1)} %compare_and_fusion.3), kind=kOutput, calls=%fused_computation.68.clone.1 | convolution fusion | flops 11138560 | bytes 1509376 | tf_op jit(solution)/shard_map/while/body/eval_jaxpr/qhr,kr->qhk/dot_general | solution.py:60
  54.9 3.8 %fusion.64 = f32[64,40,64]{0,2,1:T(8,128)} fusion(f32[64,40,64]{0,2,1:T(8,128)} %get-tuple-element.255, bf16[256,40,64]{0,2,1:T(8,128)(2,1)} %get-tuple-element.274, f32[64,40,64]{0,2,1:T(8,128)S(1)} %get-tuple-element.234, f32[64,40]{0,1:T(8,128)S(1)} %get-tuple-element.236, f32[64,40]{0,1:T(8,128)S(1)} %max.4, ...), kind=kOutput, calls=%fused_computation.4.clone.1 | convolution fusion | flops 105840640 | bytes 4014080 | tf_op jit(solution)/shard_map/while/body/eval_jaxpr/qhk,khd->qhd/dot_general | solution.py:67
  59.3 3.3 %collective-permute-done.1 = s32[2,64]{1,0:T(2,128)S(1)} collective-permute-done((s32[2,64]{1,0:T(2,128)S(1)}, s32[2,64]{1,0:T(2,128)S(1)}, u32[]{:S(2)}, u32[]{:S(2)}) %collective-permute-start.1) | collective-permute-done | bytes 544 | tf_op jit(solution)/shard_map/while/body/eval_jaxpr/ppermute | solution.py:76
  63.4 3.6 %convolution_bitcast_fusion.5 = f32[64,40,64]{0,2,1:T(8,128)} fusion(bf16[64,40,64]{2,0,1:T(8,128)(2,1)} %get-tuple-element.272, bf16[256,40,64]{0,2,1:T(8,128)(2,1)} %get-tuple-element.271, bf16[64,288]{1,0:T(8,128)(2,1)S(1)} %collective-permute-done), kind=kOutput, calls=%fused_computation.3.clone.1 | convolution fusion | flops 105021440 | bytes 2326528 | tf_op jit(solution)/shard_map/while/body/eval_jaxpr/qhd,khd->qhk/dot_general | solution.py:59
  67.0 1.8 %fusion.62 = (f32[64,40]{0,1:T(8,128)S(1)}, f32[64,40,64]{0,2,1:T(8,128)S(1)}) fusion(f32[64,40,64]{0,2,1:T(8,128)} %convolution_bitcast_fusion.5, bf16[64,40,32]{0,2,1:T(8,128)(2,1)} %get-tuple-element.273, bf16[64,288]{1,0:T(8,128)(2,1)S(1)} %collective-permute-done, pred[64,64]{0,1:T(8,128)(4,1)S(1)} %compare_and_fusion.3), kind=kOutput, calls=%fused_computation.68.clone.1 | convolution fusion | flops 11138560 | bytes 1509376 | tf_op jit(solution)/shard_map/while/body/eval_jaxpr/qhr,kr->qhk/dot_general | solution.py:60
  69.2 3.8 %fusion.64 = f32[64,40,64]{0,2,1:T(8,128)} fusion(f32[64,40,64]{0,2,1:T(8,128)} %get-tuple-element.255, bf16[256,40,64]{0,2,1:T(8,128)(2,1)} %get-tuple-element.274, f32[64,40,64]{0,2,1:T(8,128)S(1)} %get-tuple-element.234, f32[64,40]{0,1:T(8,128)S(1)} %get-tuple-element.236, f32[64,40]{0,1:T(8,128)S(1)} %max.4, ...), kind=kOutput, calls=%fused_computation.4.clone.1 | convolution fusion | flops 105840640 | bytes 4014080 | tf_op jit(solution)/shard_map/while/body/eval_jaxpr/qhk,khd->qhd/dot_general | solution.py:67
  73.2 3.7 %collective-permute-done.1 = s32[2,64]{1,0:T(2,128)S(1)} collective-permute-done((s32[2,64]{1,0:T(2,128)S(1)}, s32[2,64]{1,0:T(2,128)S(1)}, u32[]{:S(2)}, u32[]{:S(2)}) %collective-permute-start.1) | collective-permute-done | bytes 544 | tf_op jit(solution)/shard_map/while/body/eval_jaxpr/ppermute | solution.py:76
  77.7 3.6 %convolution_bitcast_fusion.5 = f32[64,40,64]{0,2,1:T(8,128)} fusion(bf16[64,40,64]{2,0,1:T(8,128)(2,1)} %get-tuple-element.272, bf16[256,40,64]{0,2,1:T(8,128)(2,1)} %get-tuple-element.271, bf16[64,288]{1,0:T(8,128)(2,1)S(1)} %collective-permute-done), kind=kOutput, calls=%fused_computation.3.clone.1 | convolution fusion | flops 105021440 | bytes 2326528 | tf_op jit(solution)/shard_map/while/body/eval_jaxpr/qhd,khd->qhk/dot_general | solution.py:59
  81.3 1.8 %fusion.62 = (f32[64,40]{0,1:T(8,128)S(1)}, f32[64,40,64]{0,2,1:T(8,128)S(1)}) fusion(f32[64,40,64]{0,2,1:T(8,128)} %convolution_bitcast_fusion.5, bf16[64,40,32]{0,2,1:T(8,128)(2,1)} %get-tuple-element.273, bf16[64,288]{1,0:T(8,128)(2,1)S(1)} %collective-permute-done, pred[64,64]{0,1:T(8,128)(4,1)S(1)} %compare_and_fusion.3), kind=kOutput, calls=%fused_computation.68.clone.1 | convolution fusion | flops 11138560 | bytes 1509376 | tf_op jit(solution)/shard_map/while/body/eval_jaxpr/qhr,kr->qhk/dot_general | solution.py:60
  83.6 3.8 %fusion.64 = f32[64,40,64]{0,2,1:T(8,128)} fusion(f32[64,40,64]{0,2,1:T(8,128)} %get-tuple-element.255, bf16[256,40,64]{0,2,1:T(8,128)(2,1)} %get-tuple-element.274, f32[64,40,64]{0,2,1:T(8,128)S(1)} %get-tuple-element.234, f32[64,40]{0,1:T(8,128)S(1)} %get-tuple-element.236, f32[64,40]{0,1:T(8,128)S(1)} %max.4, ...), kind=kOutput, calls=%fused_computation.4.clone.1 | convolution fusion | flops 105840640 | bytes 4014080 | tf_op jit(solution)/shard_map/while/body/eval_jaxpr/qhk,khd->qhd/dot_general | solution.py:67
  87.5 3.7 %collective-permute-done.1 = s32[2,64]{1,0:T(2,128)S(1)} collective-permute-done((s32[2,64]{1,0:T(2,128)S(1)}, s32[2,64]{1,0:T(2,128)S(1)}, u32[]{:S(2)}, u32[]{:S(2)}) %collective-permute-start.1) | collective-permute-done | bytes 544 | tf_op jit(solution)/shard_map/while/body/eval_jaxpr/ppermute | solution.py:76
  92.0 3.6 %convolution_bitcast_fusion.5 = f32[64,40,64]{0,2,1:T(8,128)} fusion(bf16[64,40,64]{2,0,1:T(8,128)(2,1)} %get-tuple-element.272, bf16[256,40,64]{0,2,1:T(8,128)(2,1)} %get-tuple-element.271, bf16[64,288]{1,0:T(8,128)(2,1)S(1)} %collective-permute-done), kind=kOutput, calls=%fused_computation.3.clone.1 | convolution fusion | flops 105021440 | bytes 2326528 | tf_op jit(solution)/shard_map/while/body/eval_jaxpr/qhd,khd->qhk/dot_general | solution.py:59
  95.6 1.8 %fusion.62 = (f32[64,40]{0,1:T(8,128)S(1)}, f32[64,40,64]{0,2,1:T(8,128)S(1)}) fusion(f32[64,40,64]{0,2,1:T(8,128)} %convolution_bitcast_fusion.5, bf16[64,40,32]{0,2,1:T(8,128)(2,1)} %get-tuple-element.273, bf16[64,288]{1,0:T(8,128)(2,1)S(1)} %collective-permute-done, pred[64,64]{0,1:T(8,128)(4,1)S(1)} %compare_and_fusion.3), kind=kOutput, calls=%fused_computation.68.clone.1 | convolution fusion | flops 11138560 | bytes 1509376 | tf_op jit(solution)/shard_map/while/body/eval_jaxpr/qhr,kr->qhk/dot_general | solution.py:60
  97.9 3.8 %fusion.64 = f32[64,40,64]{0,2,1:T(8,128)} fusion(f32[64,40,64]{0,2,1:T(8,128)} %get-tuple-element.255, bf16[256,40,64]{0,2,1:T(8,128)(2,1)} %get-tuple-element.274, f32[64,40,64]{0,2,1:T(8,128)S(1)} %get-tuple-element.234, f32[64,40]{0,1:T(8,128)S(1)} %get-tuple-element.236, f32[64,40]{0,1:T(8,128)S(1)} %max.4, ...), kind=kOutput, calls=%fused_computation.4.clone.1 | convolution fusion | flops 105840640 | bytes 4014080 | tf_op jit(solution)/shard_map/while/body/eval_jaxpr/qhk,khd->qhd/dot_general | solution.py:67
  101.8 3.7 %collective-permute-done.1 = s32[2,64]{1,0:T(2,128)S(1)} collective-permute-done((s32[2,64]{1,0:T(2,128)S(1)}, s32[2,64]{1,0:T(2,128)S(1)}, u32[]{:S(2)}, u32[]{:S(2)}) %collective-permute-start.1) | collective-permute-done | bytes 544 | tf_op jit(solution)/shard_map/while/body/eval_jaxpr/ppermute | solution.py:76
  106.3 3.6 %convolution_bitcast_fusion.5 = f32[64,40,64]{0,2,1:T(8,128)} fusion(bf16[64,40,64]{2,0,1:T(8,128)(2,1)} %get-tuple-element.272, bf16[256,40,64]{0,2,1:T(8,128)(2,1)} %get-tuple-element.271, bf16[64,288]{1,0:T(8,128)(2,1)S(1)} %collective-permute-done), kind=kOutput, calls=%fused_computation.3.clone.1 | convolution fusion | flops 105021440 | bytes 2326528 | tf_op jit(solution)/shard_map/while/body/eval_jaxpr/qhd,khd->qhk/dot_general | solution.py:59
  109.9 1.8 %fusion.62 = (f32[64,40]{0,1:T(8,128)S(1)}, f32[64,40,64]{0,2,1:T(8,128)S(1)}) fusion(f32[64,40,64]{0,2,1:T(8,128)} %convolution_bitcast_fusion.5, bf16[64,40,32]{0,2,1:T(8,128)(2,1)} %get-tuple-element.273, bf16[64,288]{1,0:T(8,128)(2,1)S(1)} %collective-permute-done, pred[64,64]{0,1:T(8,128)(4,1)S(1)} %compare_and_fusion.3), kind=kOutput, calls=%fused_computation.68.clone.1 | convolution fusion | flops 11138560 | bytes 1509376 | tf_op jit(solution)/shard_map/while/body/eval_jaxpr/qhr,kr->qhk/dot_general | solution.py:60
  112.2 3.8 %fusion.64 = f32[64,40,64]{0,2,1:T(8,128)} fusion(f32[64,40,64]{0,2,1:T(8,128)} %get-tuple-element.255, bf16[256,40,64]{0,2,1:T(8,128)(2,1)} %get-tuple-element.274, f32[64,40,64]{0,2,1:T(8,128)S(1)} %get-tuple-element.234, f32[64,40]{0,1:T(8,128)S(1)} %get-tuple-element.236, f32[64,40]{0,1:T(8,128)S(1)} %max.4, ...), kind=kOutput, calls=%fused_computation.4.clone.1 | convolution fusion | flops 105840640 | bytes 4014080 | tf_op jit(solution)/shard_map/while/body/eval_jaxpr/qhk,khd->qhd/dot_general | solution.py:67
  116.1 3.7 %collective-permute-done.1 = s32[2,64]{1,0:T(2,128)S(1)} collective-permute-done((s32[2,64]{1,0:T(2,128)S(1)}, s32[2,64]{1,0:T(2,128)S(1)}, u32[]{:S(2)}, u32[]{:S(2)}) %collective-permute-start.1) | collective-permute-done | bytes 544 | tf_op jit(solution)/shard_map/while/body/eval_jaxpr/ppermute | solution.py:76
  120.6 3.6 %convolution_bitcast_fusion.5 = f32[64,40,64]{0,2,1:T(8,128)} fusion(bf16[64,40,64]{2,0,1:T(8,128)(2,1)} %get-tuple-element.272, bf16[256,40,64]{0,2,1:T(8,128)(2,1)} %get-tuple-element.271, bf16[64,288]{1,0:T(8,128)(2,1)S(1)} %collective-permute-done), kind=kOutput, calls=%fused_computation.3.clone.1 | convolution fusion | flops 105021440 | bytes 2326528 | tf_op jit(solution)/shard_map/while/body/eval_jaxpr/qhd,khd->qhk/dot_general | solution.py:59
  124.2 1.8 %fusion.62 = (f32[64,40]{0,1:T(8,128)S(1)}, f32[64,40,64]{0,2,1:T(8,128)S(1)}) fusion(f32[64,40,64]{0,2,1:T(8,128)} %convolution_bitcast_fusion.5, bf16[64,40,32]{0,2,1:T(8,128)(2,1)} %get-tuple-element.273, bf16[64,288]{1,0:T(8,128)(2,1)S(1)} %collective-permute-done, pred[64,64]{0,1:T(8,128)(4,1)S(1)} %compare_and_fusion.3), kind=kOutput, calls=%fused_computation.68.clone.1 | convolution fusion | flops 11138560 | bytes 1509376 | tf_op jit(solution)/shard_map/while/body/eval_jaxpr/qhr,kr->qhk/dot_general | solution.py:60
  126.5 3.8 %fusion.64 = f32[64,40,64]{0,2,1:T(8,128)} fusion(f32[64,40,64]{0,2,1:T(8,128)} %get-tuple-element.255, bf16[256,40,64]{0,2,1:T(8,128)(2,1)} %get-tuple-element.274, f32[64,40,64]{0,2,1:T(8,128)S(1)} %get-tuple-element.234, f32[64,40]{0,1:T(8,128)S(1)} %get-tuple-element.236, f32[64,40]{0,1:T(8,128)S(1)} %max.4, ...), kind=kOutput, calls=%fused_computation.4.clone.1 | convolution fusion | flops 105840640 | bytes 4014080 | tf_op jit(solution)/shard_map/while/body/eval_jaxpr/qhk,khd->qhd/dot_general | solution.py:67
  130.2 1.5 %divide_convert_fusion = bf16[64,40,64]{0,2,1:T(8,128)(2,1)S(1)} fusion(f32[64,40,64]{0,2,1:T(8,128)} %get-tuple-element.68, f32[64,40]{0,1:T(8,128)S(1)} %get-tuple-element.69), kind=kLoop, calls=%fused_computation.32 | loop fusion | flops 327680 | bytes 993280 | tf_op jit(solution)/shard_map/convert_element_type | solution.py:81
  131.7 7.9 %convolution_convert_fusion.2 = bf16[64,2560]{1,0:T(8,128)(2,1)} fusion(bf16[64,2560]{0,1:T(8,128)(2,1)S(1)} %bitcast.81, bf16[2560,2560]{1,0:T(8,128)(2,1)} %param.25), kind=kOutput, calls=%fused_computation.22 | convolution fusion | flops 839024640 | bytes 13762560 | tf_op jit(solution)/shard_map/dot_general | solution.py:82
  (108 shorter events, 11.0 us)
Async XLA Ops:
  0.0 3.3 %copy-start = (bf16[768,1280]{1,0:T(8,128)(2,1)S(1)}, bf16[768,1280]{1,0:T(8,128)(2,1)}, u32[]{:S(2)}) copy-start(bf16[768,1280]{1,0:T(8,128)(2,1)} %param.20) | copy-start | bytes 5898244
  0.0 3.3 %copy-start.7 = (bf16[768]{0:T(1024)(128)(2,1)S(1)}, bf16[768]{0:T(1024)(128)(2,1)}, u32[]{:S(2)}) copy-start(bf16[768]{0:T(1024)(128)(2,1)} %param.26) | copy-start | bytes 4612
  0.0 4.3 %copy-start.3 = (bf16[64,2560]{1,0:T(8,128)(2,1)S(1)}, bf16[64,2560]{1,0:T(8,128)(2,1)}, u32[]{:S(2)}) copy-start(bf16[64,2560]{1,0:T(8,128)(2,1)} %param.15) | copy-start | bytes 983044
  0.0 4.3 %copy-start.4 = (bf16[2560,32]{0,1:T(8,128)(2,1)S(1)}, bf16[2560,32]{0,1:T(8,128)(2,1)}, u32[]{:S(2)}) copy-start(bf16[2560,32]{0,1:T(8,128)(2,1)} %param.22) | copy-start | bytes 491524
  0.0 4.5 %copy-start.6 = (s32[64]{0:T(128)S(1)}, s32[64]{0:T(128)}, u32[]{:S(2)}) copy-start(s32[64]{0:T(128)} %param.16) | copy-start | bytes 772
  3.3 2.1 %copy-start.2 = (bf16[768,2560]{1,0:T(8,128)(2,1)S(1)}, bf16[768,2560]{1,0:T(8,128)(2,1)}, u32[]{:S(2)}) copy-start(bf16[768,2560]{1,0:T(8,128)(2,1)} %param.19) | copy-start | bytes 11796484
  6.3 2.4 %copy-start.8 = (bf16[256]{0:T(256)(128)(2,1)S(1)}, bf16[256]{0:T(256)(128)(2,1)}, u32[]{:S(2)}) copy-start(bf16[256]{0:T(256)(128)(2,1)} %param.27) | copy-start | bytes 1540
  6.7 4.6 %copy-start.1 = (bf16[64,40,64]{2,1,0:T(8,128)(2,1)}, bf16[64,40,64]{2,1,0:T(8,128)(2,1)S(1)}, u32[]{:S(2)}) copy-start(bf16[64,40,64]{2,1,0:T(8,128)(2,1)S(1)} %reshape.189) | copy-start | bytes 983044
  18.4 2.4 %copy-start.5 = (f32[64,40]{0,1:T(8,128)S(1)}, f32[64,40]{0,1:T(8,128)}, u32[]{:S(2)}) copy-start(f32[64,40]{0,1:T(8,128)} %get-tuple-element.138) | copy-start | bytes 30724
  29.0 5.0 %collective-permute-start.1 = (s32[2,64]{1,0:T(2,128)S(1)}, s32[2,64]{1,0:T(2,128)S(1)}, u32[]{:S(2)}, u32[]{:S(2)}) collective-permute-start(s32[2,64]{1,0:T(2,128)S(1)} %get-tuple-element.252), channel_id=1, source_target_pairs={{0,1},{1,2},{2,3},{3,4},{4,5},{5,6},{6,7},{7,0}} | collective-permute-start | bytes 1544 | tf_op jit(solution)/shard_map/while/body/eval_jaxpr/ppermute | solution.py:76
  29.8 4.9 %collective-permute-start = (bf16[64,288]{1,0:T(8,128)(2,1)S(1)}, bf16[64,288]{1,0:T(8,128)(2,1)S(1)}, u32[]{:S(2)}, u32[]{:S(2)}) collective-permute-start(bf16[64,288]{1,0:T(8,128)(2,1)S(1)} %get-tuple-element.251), channel_id=1, source_target_pairs={{0,1},{1,2},{2,3},{3,4},{4,5},{5,6},{6,7},{7,0}} | collective-permute-start | bytes 110600 | tf_op jit(solution)/shard_map/while/body/eval_jaxpr/ppermute | solution.py:75
  44.4 3.9 %collective-permute-start.1 = (s32[2,64]{1,0:T(2,128)S(1)}, s32[2,64]{1,0:T(2,128)S(1)}, u32[]{:S(2)}, u32[]{:S(2)}) collective-permute-start(s32[2,64]{1,0:T(2,128)S(1)} %get-tuple-element.252), channel_id=1, source_target_pairs={{0,1},{1,2},{2,3},{3,4},{4,5},{5,6},{6,7},{7,0}} | collective-permute-start | bytes 1544 | tf_op jit(solution)/shard_map/while/body/eval_jaxpr/ppermute | solution.py:76
  44.4 4.7 %collective-permute-start = (bf16[64,288]{1,0:T(8,128)(2,1)S(1)}, bf16[64,288]{1,0:T(8,128)(2,1)S(1)}, u32[]{:S(2)}, u32[]{:S(2)}) collective-permute-start(bf16[64,288]{1,0:T(8,128)(2,1)S(1)} %get-tuple-element.251), channel_id=1, source_target_pairs={{0,1},{1,2},{2,3},{3,4},{4,5},{5,6},{6,7},{7,0}} | collective-permute-start | bytes 110600 | tf_op jit(solution)/shard_map/while/body/eval_jaxpr/ppermute | solution.py:75
  58.7 3.9 %collective-permute-start.1 = (s32[2,64]{1,0:T(2,128)S(1)}, s32[2,64]{1,0:T(2,128)S(1)}, u32[]{:S(2)}, u32[]{:S(2)}) collective-permute-start(s32[2,64]{1,0:T(2,128)S(1)} %get-tuple-element.252), channel_id=1, source_target_pairs={{0,1},{1,2},{2,3},{3,4},{4,5},{5,6},{6,7},{7,0}} | collective-permute-start | bytes 1544 | tf_op jit(solution)/shard_map/while/body/eval_jaxpr/ppermute | solution.py:76
  58.7 4.7 %collective-permute-start = (bf16[64,288]{1,0:T(8,128)(2,1)S(1)}, bf16[64,288]{1,0:T(8,128)(2,1)S(1)}, u32[]{:S(2)}, u32[]{:S(2)}) collective-permute-start(bf16[64,288]{1,0:T(8,128)(2,1)S(1)} %get-tuple-element.251), channel_id=1, source_target_pairs={{0,1},{1,2},{2,3},{3,4},{4,5},{5,6},{6,7},{7,0}} | collective-permute-start | bytes 110600 | tf_op jit(solution)/shard_map/while/body/eval_jaxpr/ppermute | solution.py:75
  73.0 3.9 %collective-permute-start.1 = (s32[2,64]{1,0:T(2,128)S(1)}, s32[2,64]{1,0:T(2,128)S(1)}, u32[]{:S(2)}, u32[]{:S(2)}) collective-permute-start(s32[2,64]{1,0:T(2,128)S(1)} %get-tuple-element.252), channel_id=1, source_target_pairs={{0,1},{1,2},{2,3},{3,4},{4,5},{5,6},{6,7},{7,0}} | collective-permute-start | bytes 1544 | tf_op jit(solution)/shard_map/while/body/eval_jaxpr/ppermute | solution.py:76
  73.0 4.7 %collective-permute-start = (bf16[64,288]{1,0:T(8,128)(2,1)S(1)}, bf16[64,288]{1,0:T(8,128)(2,1)S(1)}, u32[]{:S(2)}, u32[]{:S(2)}) collective-permute-start(bf16[64,288]{1,0:T(8,128)(2,1)S(1)} %get-tuple-element.251), channel_id=1, source_target_pairs={{0,1},{1,2},{2,3},{3,4},{4,5},{5,6},{6,7},{7,0}} | collective-permute-start | bytes 110600 | tf_op jit(solution)/shard_map/while/body/eval_jaxpr/ppermute | solution.py:75
  87.3 3.9 %collective-permute-start.1 = (s32[2,64]{1,0:T(2,128)S(1)}, s32[2,64]{1,0:T(2,128)S(1)}, u32[]{:S(2)}, u32[]{:S(2)}) collective-permute-start(s32[2,64]{1,0:T(2,128)S(1)} %get-tuple-element.252), channel_id=1, source_target_pairs={{0,1},{1,2},{2,3},{3,4},{4,5},{5,6},{6,7},{7,0}} | collective-permute-start | bytes 1544 | tf_op jit(solution)/shard_map/while/body/eval_jaxpr/ppermute | solution.py:76
  87.3 4.7 %collective-permute-start = (bf16[64,288]{1,0:T(8,128)(2,1)S(1)}, bf16[64,288]{1,0:T(8,128)(2,1)S(1)}, u32[]{:S(2)}, u32[]{:S(2)}) collective-permute-start(bf16[64,288]{1,0:T(8,128)(2,1)S(1)} %get-tuple-element.251), channel_id=1, source_target_pairs={{0,1},{1,2},{2,3},{3,4},{4,5},{5,6},{6,7},{7,0}} | collective-permute-start | bytes 110600 | tf_op jit(solution)/shard_map/while/body/eval_jaxpr/ppermute | solution.py:75
  101.6 3.9 %collective-permute-start.1 = (s32[2,64]{1,0:T(2,128)S(1)}, s32[2,64]{1,0:T(2,128)S(1)}, u32[]{:S(2)}, u32[]{:S(2)}) collective-permute-start(s32[2,64]{1,0:T(2,128)S(1)} %get-tuple-element.252), channel_id=1, source_target_pairs={{0,1},{1,2},{2,3},{3,4},{4,5},{5,6},{6,7},{7,0}} | collective-permute-start | bytes 1544 | tf_op jit(solution)/shard_map/while/body/eval_jaxpr/ppermute | solution.py:76
  101.6 4.7 %collective-permute-start = (bf16[64,288]{1,0:T(8,128)(2,1)S(1)}, bf16[64,288]{1,0:T(8,128)(2,1)S(1)}, u32[]{:S(2)}, u32[]{:S(2)}) collective-permute-start(bf16[64,288]{1,0:T(8,128)(2,1)S(1)} %get-tuple-element.251), channel_id=1, source_target_pairs={{0,1},{1,2},{2,3},{3,4},{4,5},{5,6},{6,7},{7,0}} | collective-permute-start | bytes 110600 | tf_op jit(solution)/shard_map/while/body/eval_jaxpr/ppermute | solution.py:75
  115.9 3.9 %collective-permute-start.1 = (s32[2,64]{1,0:T(2,128)S(1)}, s32[2,64]{1,0:T(2,128)S(1)}, u32[]{:S(2)}, u32[]{:S(2)}) collective-permute-start(s32[2,64]{1,0:T(2,128)S(1)} %get-tuple-element.252), channel_id=1, source_target_pairs={{0,1},{1,2},{2,3},{3,4},{4,5},{5,6},{6,7},{7,0}} | collective-permute-start | bytes 1544 | tf_op jit(solution)/shard_map/while/body/eval_jaxpr/ppermute | solution.py:76
  115.9 4.7 %collective-permute-start = (bf16[64,288]{1,0:T(8,128)(2,1)S(1)}, bf16[64,288]{1,0:T(8,128)(2,1)S(1)}, u32[]{:S(2)}, u32[]{:S(2)}) collective-permute-start(bf16[64,288]{1,0:T(8,128)(2,1)S(1)} %get-tuple-element.251), channel_id=1, source_target_pairs={{0,1},{1,2},{2,3},{3,4},{4,5},{5,6},{6,7},{7,0}} | collective-permute-start | bytes 110600 | tf_op jit(solution)/shard_map/while/body/eval_jaxpr/ppermute | solution.py:75
where the time goes:
time: 141 us; the launch traced here: 140 us
  matrix products  88.5 us (63%)
  waiting for transfers between devices  22.2 us (16%)
  other arithmetic  14.2 us (10%)
  local copies, waits for them, and re-layouts  7.74 us (5%)
  starting transfers between devices  6.26 us (4%)
    dot_general x8, matrix products, attend_block(): jnp.einsum('qhk,khd->qhd', weights.astype(jnp.bfloat16), v_blk, preferred...  29.6 us
    dot_general x8, matrix products, attend_block(): jnp.einsum('qhd,khd->qhk', q_nope, k_nope, preferred_element_type=jnp.flo...  29 us
    ppermute x7, waiting for transfers between devices, hop_step(): ids_blk = lax.ppermute(ids_blk, 'ctx', shift_pairs)  22.1 us
    dot_general x8, matrix products, attend_block(): jnp.einsum('qhr,kr->qhk', q_rope, lat_blk[:, kv_rank:], preferred_element...  14.7 us
    dot_general x1, matrix products, per_device(): jnp.dot(attn_out, w_out, preferred_element_type=jnp.float32)  7.87 us
    and x8, other arithmetic, attend_block(): (ids_blk[0][None, :] <= pos_rows[:, None]) & (ids_blk[1][None, :] == seg_...  5.96 us
    ppermute x7, starting transfers between devices, hop_step(): lat_blk = lax.ppermute(lat_blk, 'ctx', shift_pairs)  5.38 us
    unnamed x20, local copies, waits for them, and re-layouts  4.94 us
  transfers between devices with their start and end apart: 14, of which 7 were waited for; matrix products, arithmetic and copies ran while one was open for 4% of the time, Pallas kernels for 0%

commit v1 on v0

v1 whole, which is shorter than its diff:
```python
import functools
import math

import numpy as np
import jax
import jax.numpy as jnp
from jax import lax
from jax.experimental import pallas as pl
from jax.experimental.pallas import tpu as pltpu
from jax.sharding import PartitionSpec as P

NORM_EPS = 1e-6
MESH = pl.DeviceIdType.MESH
F32 = jnp.float32
BF16 = jnp.bfloat16
GROUP_HEADS = 4


def rms_rows(vals, gain):
    mean_sq = jnp.mean(vals * vals, axis=-1, keepdims=True)
    return (vals * lax.rsqrt(mean_sq + NORM_EPS) * gain.astype(F32)).astype(BF16)


def dot_nn(a, b):
    return lax.dot_general(a, b, (((1,), (0,)), ((), ())), preferred_element_type=F32)


def dot_nt(a, b):
    return lax.dot_general(a, b, (((1,), (1,)), ((), ())), preferred_element_type=F32)


def dot_tn(a, b):
    return lax.dot_general(a, b, (((0,), (0,)), ((), ())), preferred_element_type=F32)


def kernel(n, x_hbm, pos_hbm, wdq_hbm, wuq_hbm, wqr_hbm, wdkv_hbm, wkr_hbm, wuk_hbm, wuv_hbm, wout_hbm, gq_hbm, gkv_hbm,
           y_ref, x, pos, wdq, wuq, wqr, wdkv, wkr, wuk, wuv, wout, gq, gkv,
           lat, gath, bias, qn_s, qr_s, kn_s, v_s, krep_s, o_s, load_sem, send_sem, recv_sem):
    me = lax.axis_index('ctx')
    rows = x.shape[0]
    half = rows // 2
    rank = wdkv.shape[1]
    rope = wkr.shape[0]
    num_heads = wqr.shape[1] // rope
    nope = wuq.shape[1] // num_heads
    keys = n * rows
    gw = GROUP_HEADS * nope
    rw = GROUP_HEADS * rope
    lanes = GROUP_HEADS * rows
    groups = num_heads // GROUP_HEADS

    barrier = pltpu.get_barrier_semaphore()
    for j in range(1, n):
        pl.semaphore_signal(barrier, inc=1, device_id={'ctx': lax.rem(me + j, n)}, device_id_type=MESH)

    loads = []

    def load(src, dst):
        copy = pltpu.make_async_copy(src, dst, load_sem.at[len(loads)])
        copy.start()
        loads.append(copy)
        return copy

    def load_cols(src, dst, width):
        return [load(src.at[:, pl.ds(c, width)], dst.at[:, pl.ds(c, width)]) for c in range(0, src.shape[1], width)]

    def load_rows(src, dst, height):
        return [load(src.at[pl.ds(c, height), :], dst.at[pl.ds(c, height), :]) for c in range(0, src.shape[0], height)]

    ld_pos = load(pos_hbm, pos)
    ld_x = load(x_hbm, x)
    ld_dkv = load_rows(wdkv_hbm, wdkv, 1280)
    ld_kr = load(wkr_hbm, wkr)
    ld_gkv = load(gkv_hbm, gkv)
    ld_dq = load_rows(wdq_hbm, wdq, 640)
    ld_gq = load(gq_hbm, gq)
    ld_uq = load_rows(wuq_hbm, wuq, 256)
    ld_qr = load_rows(wqr_hbm, wqr, 384)
    ld_uk = load(wuk_hbm, wuk)
    ld_uv = load(wuv_hbm, wuv)
    ld_out = load_rows(wout_hbm, wout, 256)

    ld_pos.wait()
    pos_row = pos[...]
    freq_iota = lax.broadcasted_iota(jnp.int32, (rope // 2, rows), 0)
    inv_freq = jnp.zeros((rope // 2, rows), F32)
    for i in range(rope // 2):
        inv_freq = jnp.where(freq_iota == i, np.float32(10000.0 ** (-2.0 * i / rope)), inv_freq)
    angles = pos_row.astype(F32) * inv_freq
    reps = 128 // (rope // 2)

    def table(vals):
        tall = jnp.concatenate([vals] * reps, axis=0)
        wide = jnp.concatenate([tall, tall], axis=1)
        return jnp.transpose(wide)[:rows, :]

    cos_t = table(jnp.cos(angles))
    sin_t = table(jnp.sin(angles))
    lane = lax.broadcasted_iota(jnp.int32, (rows, 128), 1)
    lead = lax.rem(lane, rope) < rope // 2
    sin_t = jnp.where(lead, -sin_t, sin_t)

    def rope128(a):
        other = jnp.where(lead, pltpu.roll(a, 128 - rope // 2, 1), pltpu.roll(a, rope // 2, 1))
        return a * cos_t + other * sin_t

    pos_l = jnp.concatenate([pos_row] * GROUP_HEADS, axis=1)
    q_in = lax.rem(lax.broadcasted_iota(jnp.int32, (1, lanes), 1), rows)
    q_tok = jnp.where(q_in < half, half * me + q_in, half * (2 * n - 1 - me) + q_in - half)
    q_first = q_tok - pos_l
    for j in range(n):
        r = lax.broadcasted_iota(jnp.int32, (rows, lanes), 0)
        k_tok = jnp.where(r < half, half * j + r, half * (2 * n - 1 - j) + r - half)
        ok = (k_tok <= q_tok) & (k_tok >= q_first)
        bias[pl.ds(j * rows, rows), :] = jnp.where(ok, jnp.inf, -jnp.inf)

    ld_x.wait()
    for c in ld_dkv:
        c.wait()
    ld_kr.wait()
    ld_gkv.wait()
    xv = x[...]
    c_kv = rms_rows(dot_nn(xv, wdkv[...]), gkv[...])
    kr = dot_nt(xv, wkr[...])
    kr = rope128(jnp.concatenate([kr] * (128 // rope), axis=1))
    pack = kr[0:16, :]
    lane16 = lax.broadcasted_iota(jnp.int32, (16, 128), 1) // rope
    for b in range(1, rows // 16):
        pack = jnp.where(lane16 == b, kr[16 * b:16 * b + 16, :], pack)
    pack = pack.astype(BF16)
    lat[0:rows, :] = c_kv[:, :128]
    lat[rows:2 * rows, :] = c_kv[:, 128:]
    lat[2 * rows:2 * rows + 16, :] = pack
    gath[me, 0:rows, :] = c_kv[:, :128]
    gath[me, rows:2 * rows, :] = c_kv[:, 128:]
    gath[me, 2 * rows:2 * rows + 16, :] = pack

    pl.semaphore_wait(barrier, n - 1)
    sends = []
    for j in range(1, n):
        peer = lax.rem(me + j, n)
        copy = pltpu.make_async_remote_copy(
            src_ref=lat, dst_ref=gath.at[me], send_sem=send_sem.at[j - 1], recv_sem=recv_sem.at[j - 1],
            device_id={'ctx': peer}, device_id_type=MESH)
        copy.start()
        sends.append(copy)

    for c in ld_dq:
        c.wait()
    ld_gq.wait()
    c_q = rms_rows(dot_nn(xv, wdq[...]), gq[...])
    for c in ld_uq:
        c.wait()
    for c in range(0, wuq.shape[1], 512):
        qn_s[:, c:c + 512] = dot_nn(c_q, wuq[:, c:c + 512]).astype(BF16)
    for c in ld_qr:
        c.wait()
    for c in range(0, wqr.shape[1], 256):
        a = dot_nn(c_q, wqr[:, c:c + 256])
        qr_s[:, c:c + 128] = rope128(a[:, :128]).astype(BF16)
        qr_s[:, c + 128:c + 256] = rope128(a[:, 128:]).astype(BF16)

    for copy in sends:
        copy.wait()
    ld_uk.wait()
    ld_uv.wait()
    c_all = jnp.concatenate([gath[:, 0:rows, :].reshape(keys, 128), gath[:, rows:2 * rows, :].reshape(keys, 128)], axis=1)
    spread_r = lax.broadcasted_iota(jnp.int32, (128, 512), 0)
    spread_c = lax.broadcasted_iota(jnp.int32, (128, 512), 1)
    spread = (spread_r == rope * (spread_c // 128) + lax.rem(spread_c, rope)).astype(F32).astype(BF16)
    wide = dot_nn(gath[:, 2 * rows:2 * rows + 16, :].reshape(n * 16, 128), spread).astype(BF16)
    for b in range(rows // 16):
        for j in range(n):
            krep_s[j * rows + 16 * b:j * rows + 16 * b + 16, :] = wide[16 * j:16 * j + 16, 128 * b:128 * b + 128]
    for c in range(0, wuk.shape[1], gw):
        kn_s[:, c:c + gw] = dot_nn(c_all, wuk[:, c:c + gw]).astype(BF16)
    for c in range(0, wuv.shape[1], gw):
        v_s[:, c:c + gw] = dot_nn(c_all, wuv[:, c:c + gw]).astype(BF16)

    scale2 = (nope + rope) ** -0.5 * math.log2(math.e)
    lane_n = lax.broadcasted_iota(jnp.int32, (1, gw), 1) // nope
    lane_r = lax.broadcasted_iota(jnp.int32, (1, rw), 1) // rope
    mask_n = [(lane_n == h).astype(F32).astype(BF16) for h in range(GROUP_HEADS)]
    mask_r = [(lane_r == h).astype(F32).astype(BF16) for h in range(GROUP_HEADS)]
    low = lax.broadcasted_iota(jnp.int32, (rows, 128), 1) < nope

    def group(g):
        qn = qn_s[:, g * gw:(g + 1) * gw]
        qr = qr_s[:, g * rw:(g + 1) * rw]
        qn_bd = jnp.concatenate([qn * mask_n[h] for h in range(GROUP_HEADS)], axis=0)
        qr_bd = jnp.concatenate([qr * mask_r[h] for h in range(GROUP_HEADS)], axis=0)
        s = dot_nt(kn_s[:, g * gw:(g + 1) * gw], qn_bd) + dot_nt(krep_s[...], qr_bd)
        s = jnp.minimum(s, bias[...])
        m = jnp.max(s, axis=0, keepdims=True)
        p = jnp.exp2((s - m) * scale2)
        inv = 1.0 / jnp.sum(p, axis=0, keepdims=True)
        o = dot_tn(p.astype(BF16), v_s[:, g * gw:(g + 1) * gw])
        inv_t = jnp.transpose(jnp.broadcast_to(inv, (128, lanes)))
        for t in range(gw // 128):
            first, second = 2 * t * rows, (2 * t + 1) * rows
            part = jnp.where(low,
                             o[first:first + rows, 128 * t:128 * t + 128] * inv_t[first:first + rows, :],
                             o[second:second + rows, 128 * t:128 * t + 128] * inv_t[second:second + rows, :])
            o_s[:, g * gw + 128 * t:g * gw + 128 * t + 128] = part.astype(BF16)

    for g in range(groups):
        group(g)

    for c in ld_out:
        c.wait()
    ov = o_s[...]
    for c in range(0, wout.shape[1], 512):
        y_ref[:, c:c + 512] = dot_nn(ov, wout[:, c:c + 512]).astype(BF16)


def solution(mesh):
    n = mesh.shape['ctx']
    row_spec = P(('dp', 'ctx'), None)
    id_spec = P(('dp', 'ctx'))

    def per_device(x_rows, pos_rows, seg_rows, w_dq, w_uq, w_qr, w_dkv, w_kr, w_uk, w_uv, w_out, gain_q, gain_kv):
        rows, d_model = x_rows.shape
        keys = n * rows
        operands = (x_rows, pos_rows.reshape(1, rows), w_dq, w_uq, w_qr, w_dkv, w_kr.T, w_uk, w_uv, w_out,
                    gain_q.reshape(1, -1), gain_kv.reshape(1, -1))
        vm = lambda a: pltpu.VMEM(a.shape, a.dtype)
        return pl.pallas_call(
            functools.partial(kernel, n),
            out_shape=jax.ShapeDtypeStruct((rows, w_out.shape[1]), BF16),
            in_specs=[pl.BlockSpec(memory_space=pl.ANY)] * len(operands),
            out_specs=pl.BlockSpec(memory_space=pltpu.VMEM),
            scratch_shapes=[vm(a) for a in operands] + [
                pltpu.VMEM((2 * rows + 16, 128), BF16),
                pltpu.VMEM((n, 2 * rows + 16, 128), BF16),
                pltpu.VMEM((keys, GROUP_HEADS * rows), F32),
                pltpu.VMEM((rows, w_uq.shape[1]), BF16),
                pltpu.VMEM((rows, w_qr.shape[1]), BF16),
                pltpu.VMEM((keys, w_uk.shape[1]), BF16),
                pltpu.VMEM((keys, w_uv.shape[1]), BF16),
                pltpu.VMEM((keys, 128), BF16),
                pltpu.VMEM((rows, w_out.shape[0]), BF16),
                pltpu.SemaphoreType.DMA((40,)),
                pltpu.SemaphoreType.DMA((n - 1,)),
                pltpu.SemaphoreType.DMA((n - 1,)),
            ],
            compiler_params=pltpu.CompilerParams(collective_id=0, has_side_effects=True, vmem_limit_bytes=62 * 1024 * 1024),
        )(*operands)

    return jax.shard_map(per_device, mesh=mesh, in_specs=(row_spec, id_spec, id_spec) + (P(),) * 10, out_specs=row_spec, check_vma=False)
```

time: 141 us -> 24.6 us (0.17)
  matrix products: 88.5 us -> 0 us
  waiting for transfers between devices: 22.2 us -> 0 us
  Pallas kernels: 0 us -> 20.3 us
  other arithmetic: 14.2 us -> 0 us
  starting transfers between devices: 6.26 us -> 0 us
  local copies, waits for them, and re-layouts: 7.74 us -> 4.22 us
    dot_general x30 -> x0, matrix products: 88.5 us -> none  [the longest x8 29.6 us: attend_block(): jnp.einsum('qhk,khd->qhd', weights.astype(jnp.bfloat16), v_blk, preferred...]
    ppermute x14 -> x0, waiting for transfers between devices: 22.2 us -> none  [the longest x7 22.1 us: hop_step(): ids_blk = lax.ppermute(ids_blk, 'ctx', shift_pairs)]
    pallas_call x0 -> x1, Pallas kernels: none -> 20.3 us  [per_device(): pl.pallas_call(functools.partial(kernel, n), out_shape=jax.ShapeDtypeStru...]
    ppermute x14 -> x0, starting transfers between devices: 6.26 us -> none  [the longest x7 5.38 us: hop_step(): lat_blk = lax.ppermute(lat_blk, 'ctx', shift_pairs)]
    and x8 -> x0, other arithmetic: 5.96 us -> none  [attend_block(): (ids_blk[0][None, :] <= pos_rows[:, None]) & (ids_blk[1][None, :] == seg_...]
    unnamed x20 -> x1, local copies, waits for them, and re-layouts: 4.94 us -> 1.72 us
    reduce_sum x8 -> x0, other arithmetic: 2.56 us -> none  [attend_block(): run_sum = run_sum * rescale + jnp.sum(weights, axis=-1)]
    another operation x4 -> x0, other arithmetic: 2.05 us -> none
  transfers between devices with their start and end apart: 14 -> 0, of which waited for: 7 -> 0; matrix products, arithmetic and copies ran while one was open for 4% -> 0% of each run, Pallas kernels for 0% -> 0%
where the time goes in v1:
time: 24.6 us; the launch traced here: 24.5 us
  Pallas kernels  20.3 us (83%)
  local copies, waits for them, and re-layouts  4.22 us (17%)
    pallas_call x1, Pallas kernels, per_device(): pl.pallas_call(functools.partial(kernel, n), out_shape=jax.ShapeDtypeStru...  20.3 us
    unnamed x1, local copies, waits for them, and re-layouts  1.72 us
    reshape x1, local copies, waits for them, and re-layouts, per_device(): gain_q.reshape(1, -1)  1.26 us
    reshape x1, local copies, waits for them, and re-layouts, per_device(): gain_kv.reshape(1, -1)  1.24 us

profile of v1, /device:TPU:0, one launch (start us, length us, event | category | flops | bytes accessed | tf_op | source)
XLA Modules:
  0.0 24.5 jit_solution(3820794741765031309)
XLA Ops:
  0.0 1.2 %reshape.11.gkv_hbm = bf16[1,256]{1,0:T(2,128)(2,1)} reshape(bf16[256]{0:T(256)(128)(2,1)} %param.24) | data formatting | bytes 1024 | tf_op jit(solution)/shard_map/reshape | solution.py:225
  1.2 1.3 %reshape.10.gq_hbm = bf16[1,768]{1,0:T(2,128)(2,1)} reshape(bf16[768]{0:T(1024)(128)(2,1)} %param.23) | data formatting | bytes 3072 | tf_op jit(solution)/shard_map/reshape | solution.py:225
  2.5 20.3 %shard_map.118 = bf16[64,2560]{1,0:T(8,128)(2,1)} custom-call(bf16[64,2560]{1,0:T(8,128)(2,1)} %x_hbm.1, s32[1,64]{1,0:T(1,128)} %bitcast.3, bf16[2560,768]{1,0:T(8,128)(2,1)} %wdq_hbm.1, bf16[768,2560]{1,0:T(8,128)(2,1)} %wuq_hbm.1, bf16[768,1280]{1,0:T(8,128)(2,1)} %wqr_hbm.1, bf16[2560,256]{1,0:T(8,128)(2,1)} %wdkv_hbm.1, bf16[32,2560]{1,0:T(8,128)(2,1)} %bitcast.2, ...), custom_call_target="tpu_custom_call" | custom-call | tf_op jit(solution)/shard_map/pallas_call | solution.py:227
  22.8 1.7 %copy.14 = bf16[64,2560]{1,0:T(8,128)(2,1)} copy(bf16[64,2560]{1,0:T(8,128)(2,1)} %shard_map.118) | data formatting | bytes 655360

commit v2 on v1

--- a/solution.py
+++ b/solution.py
@@ -120,7 +120,7 @@
     ld_kr.wait()
     ld_gkv.wait()
     xv = x[...]
-    c_kv = rms_rows(dot_nn(xv, wdkv[...]), gkv[...])
+    c_kv = rms_rows(dot_nn(xv, wdkv[...]), gkv[...].reshape(1, rank))
     kr = dot_nt(xv, wkr[...])
     kr = rope128(jnp.concatenate([kr] * (128 // rope), axis=1))
     pack = kr[0:16, :]
@@ -148,7 +148,7 @@
     for c in ld_dq:
         c.wait()
     ld_gq.wait()
-    c_q = rms_rows(dot_nn(xv, wdq[...]), gq[...])
+    c_q = rms_rows(dot_nn(xv, wdq[...]), gq[...].reshape(1, wdq.shape[1]))
     for c in ld_uq:
         c.wait()
     for c in range(0, wuq.shape[1], 512):
@@ -222,7 +222,8 @@
         rows, d_model = x_rows.shape
         keys = n * rows
         operands = (x_rows, pos_rows.reshape(1, rows), w_dq, w_uq, w_qr, w_dkv, w_kr.T, w_uk, w_uv, w_out,
-                    gain_q.reshape(1, -1), gain_kv.reshape(1, -1))
+                    gain_q, gain_kv)
+        operands = tuple(pltpu.with_memory_space_constraint(a, pltpu.HBM) for a in operands)
         vm = lambda a: pltpu.VMEM(a.shape, a.dtype)
         return pl.pallas_call(
             functools.partial(kernel, n),
@@ -243,7 +244,7 @@
                 pltpu.SemaphoreType.DMA((n - 1,)),
                 pltpu.SemaphoreType.DMA((n - 1,)),
             ],
-            compiler_params=pltpu.CompilerParams(collective_id=0, has_side_effects=True, vmem_limit_bytes=62 * 1024 * 1024),
+            compiler_params=pltpu.CompilerParams(collective_id=0, has_side_effects=True, vmem_limit_bytes=42 * 1024 * 1024),
         )(*operands)
 
     return jax.shard_map(per_device, mesh=mesh, in_specs=(row_spec, id_spec, id_spec) + (P(),) * 10, out_specs=row_spec, check_vma=False)

time: 24.6 us -> 20.4 us (0.83)
  local copies, waits for them, and re-layouts: 4.22 us -> 0.73 us
  Pallas kernels: 20.3 us -> 19.6 us
    reshape x2 -> x0, local copies, waits for them, and re-layouts: 2.51 us -> none  [the longest x1 1.26 us: per_device(): gain_q.reshape(1, -1)]
    unnamed x1, local copies, waits for them, and re-layouts: 1.72 us -> 0.73 us
    pallas_call x1, Pallas kernels: 20.3 us -> 19.6 us  [per_device(): pl.pallas_call(functools.partial(kernel, n), out_shape=jax.ShapeDtypeStru...]
where the time goes in v2:
time: 20.4 us; the launch traced here: 20.3 us
  Pallas kernels  19.6 us (96%)
  local copies, waits for them, and re-layouts  0.73 us (4%)
    pallas_call x1, Pallas kernels, per_device(): pl.pallas_call(functools.partial(kernel, n), out_shape=jax.ShapeDtypeStru...  19.6 us
    unnamed x1, local copies, waits for them, and re-layouts  0.73 us

profile of v2, /device:TPU:0, one launch (start us, length us, event | category | flops | bytes accessed | tf_op | source)
XLA Modules:
  0.0 20.3 jit_solution(15506230898618528895)
XLA Ops:
  0.0 19.6 %shard_map.118 = bf16[64,2560]{1,0:T(8,128)(2,1)S(1)} custom-call(bf16[64,2560]{1,0:T(8,128)(2,1)} %x_hbm.1, s32[1,64]{1,0:T(1,128)} %bitcast.3, bf16[2560,768]{1,0:T(8,128)(2,1)} %wdq_hbm.1, bf16[768,2560]{1,0:T(8,128)(2,1)} %wuq_hbm.1, bf16[768,1280]{1,0:T(8,128)(2,1)} %wqr_hbm.1, bf16[2560,256]{1,0:T(8,128)(2,1)} %wdkv_hbm.1, bf16[32,2560]{1,0:T(8,128)(2,1)} %bitcast.2, ...), custom_call_target="tpu_custom_call" | custom-call | tf_op jit(solution)/shard_map/pallas_call | solution.py:228
  19.6 0.7 %copy.14 = bf16[64,2560]{1,0:T(8,128)(2,1)} copy(bf16[64,2560]{1,0:T(8,128)(2,1)S(1)} %shard_map.118) | data formatting | bytes 655360

commit v3 on v2

v3 whole, which is shorter than its diff:
```python
import functools
import math

import numpy as np
import jax
import jax.numpy as jnp
from jax import lax
from jax.experimental import pallas as pl
from jax.experimental.pallas import tpu as pltpu
from jax.sharding import PartitionSpec as P

NORM_EPS = 1e-6
MESH = pl.DeviceIdType.MESH
F32 = jnp.float32
BF16 = jnp.bfloat16
LANES = 128


def rms_rows(vals, gain):
    mean_sq = jnp.mean(vals * vals, axis=-1, keepdims=True)
    return (vals * lax.rsqrt(mean_sq + NORM_EPS) * gain.astype(F32)).astype(BF16)


def dot_nn(a, b):
    return lax.dot_general(a, b, (((1,), (0,)), ((), ())), preferred_element_type=F32)


def dot_nt(a, b):
    return lax.dot_general(a, b, (((1,), (1,)), ((), ())), preferred_element_type=F32)


def dot_tt(a, b):
    return lax.dot_general(a, b, (((0,), (1,)), ((), ())), preferred_element_type=F32)


def iota(shape, axis):
    return lax.broadcasted_iota(jnp.int32, shape, axis)


def kernel(n, rows, rope, nope, x_hbm, pos_hbm, wdq_hbm, wuq_hbm, wqr_hbm, wdkv_hbm, wkr_hbm, wuk_hbm, wuv_hbm, wout_hbm,
           gq_hbm, gkv_hbm, y_ref, x, pos, wdq, wuq, wqr, wdkv, wkr, wuk, wuv, wout, gq, gkv,
           lat, gath, bias, qbd, kn_s, vt_s, m_s, l_s, acc_s, o_own, o_out, o_in, y_acc,
           load_sem, send_sem, recv_sem, pair_send, pair_recv):
    me = lax.axis_index('ctx')
    core = lax.rem(me, 2)
    chip = me // 2
    partner = me + 1 - 2 * core
    half = rows // 2
    rank = wdkv.shape[1]
    pair = 2 * rows
    cols = wuq.shape[1]
    groups = cols // LANES
    part = n // 2
    keys = part * rows
    tables = rope // 2

    barrier = pltpu.get_barrier_semaphore()
    for j in range(1, n):
        pl.semaphore_signal(barrier, inc=1, device_id={'ctx': lax.rem(me + j, n)}, device_id_type=MESH)

    loads = []

    def load(src, dst):
        copy = pltpu.make_async_copy(src, dst, load_sem.at[len(loads)])
        copy.start()
        loads.append(copy)
        return copy

    def load_rows(src, dst, height, first=0):
        return [load(src.at[pl.ds(first + c, height), :], dst.at[pl.ds(c, height), :]) for c in range(0, dst.shape[0], height)]

    mine = pl.ds(pl.multiple_of(core * rows, rows), rows)
    head_cols = pl.ds(pl.multiple_of(core * cols, LANES), cols)
    rope_cols = pl.ds(pl.multiple_of(core * wqr.shape[1], LANES), wqr.shape[1])
    ld_pos = load(pos_hbm, pos.at[core])
    ld_x = load(x_hbm, x.at[mine, :])
    ld_dkv = load_rows(wdkv_hbm, wdkv, 1280)
    ld_kr = load(wkr_hbm, wkr)
    ld_gkv = load(gkv_hbm, gkv)
    ld_dq = load_rows(wdq_hbm, wdq, 640)
    ld_gq = load(gq_hbm, gq)
    ld_uq = load(wuq_hbm.at[:, head_cols], wuq)
    ld_qr = load(wqr_hbm.at[:, rope_cols], wqr)
    ld_uk = load(wuk_hbm.at[:, head_cols], wuk)
    ld_uv = load(wuv_hbm.at[:, head_cols], wuv)
    row_a = pl.multiple_of(core * cols, LANES)
    row_b = pl.multiple_of((1 - core) * cols, LANES)
    ld_out = [load(wout_hbm.at[pl.ds(row_a + c, 256), :], wout.at[pl.ds(c, 256), :]) for c in range(0, cols, 256)]
    ld_out += [load(wout_hbm.at[pl.ds(row_b + c, 256), :], wout.at[pl.ds(cols + c, 256), :]) for c in range(0, cols, 256)]

    def rope_tables(pos_row):
        width = pos_row.shape[1]
        freq = iota((tables, width), 0)
        inv_freq = jnp.zeros((tables, width), F32)
        for i in range(tables):
            inv_freq = jnp.where(freq == i, np.float32(10000.0 ** (-2.0 * i / rope)), inv_freq)
        angles = pos_row.astype(F32) * inv_freq

        def table(vals):
            tall = jnp.concatenate([vals] * (LANES // tables), axis=0)
            if width < LANES:
                tall = jnp.concatenate([tall] * (LANES // width), axis=1)
            return jnp.transpose(tall)[:width, :]

        lead = lax.rem(iota((width, LANES), 1), rope) < tables
        cos_t, sin_t = table(jnp.cos(angles)), table(jnp.sin(angles))
        return cos_t, jnp.where(lead, -sin_t, sin_t), lead

    def rotate(a, tabs):
        cos_t, sin_t, lead = tabs
        other = jnp.where(lead, pltpu.roll(a, LANES - tables, 1), pltpu.roll(a, tables, 1))
        return a * cos_t + other * sin_t

    ld_pos.wait()
    tabs = rope_tables(pos[core])
    ld_x.wait()
    for c in ld_dkv:
        c.wait()
    ld_kr.wait()
    ld_gkv.wait()
    xv = x[mine, :]
    c_kv = rms_rows(dot_nn(xv, wdkv[...]), gkv[...].reshape(1, rank))
    kr = dot_nt(xv, wkr[...])
    kr = rotate(jnp.concatenate([kr] * (LANES // rope), axis=1), tabs)
    pack = kr[0:16, :]
    lane16 = iota((16, LANES), 1) // rope
    for b in range(1, rows // 16):
        pack = jnp.where(lane16 == b, kr[16 * b:16 * b + 16, :], pack)
    pack = pack.astype(BF16)
    lat[0:rows, :] = c_kv[:, :LANES]
    lat[rows:2 * rows, :] = c_kv[:, LANES:]
    lat[2 * rows:2 * rows + 16, :] = pack
    gath[me, 0:rows, :] = c_kv[:, :LANES]
    gath[me, rows:2 * rows, :] = c_kv[:, LANES:]
    gath[me, 2 * rows:2 * rows + 16, :] = pack

    pl.semaphore_wait(barrier, n - 1)
    sends = []
    for j in range(1, n):
        flip_chip, flip_core = j // 2, j % 2
        bit0 = lax.rem(chip, 2)
        bit1 = chip // 2
        peer_chip = (bit0 + (flip_chip % 2) * (1 - 2 * bit0)) + 2 * (bit1 + (flip_chip // 2) * (1 - 2 * bit1))
        peer = 2 * peer_chip + core + flip_core * (1 - 2 * core)
        copy = pltpu.make_async_remote_copy(
            src_ref=lat, dst_ref=gath.at[me], send_sem=send_sem.at[j - 1], recv_sem=recv_sem.at[j - 1],
            device_id={'ctx': peer}, device_id_type=MESH)
        copy.start()
        sends.append(copy)

    def to_partner(src, dst, index):
        copy = pltpu.make_async_remote_copy(
            src_ref=src, dst_ref=dst, send_sem=pair_send.at[index], recv_sem=pair_recv.at[index],
            device_id={'ctx': partner}, device_id_type=MESH)
        copy.start()
        return copy

    pair_x = to_partner(x.at[mine, :], x.at[mine, :], 0)
    pair_pos = to_partner(pos.at[core], pos.at[core], 1)
    qbd[...] = jnp.zeros_like(qbd)

    pair_pos.wait()
    pos_row = jnp.concatenate([pos[0], pos[1]], axis=1)
    tabs = rope_tables(pos_row)
    pair_x.wait()
    for c in ld_dq:
        c.wait()
    ld_gq.wait()
    c_q = rms_rows(dot_nn(x[...], wdq[...]), gq[...].reshape(1, wdq.shape[1]))
    ld_uq.wait()
    for c in range(0, cols, 256):
        q = dot_nn(c_q, wuq[:, c:c + 256]).astype(BF16)
        for t in range(2):
            qt = jnp.transpose(q[:, LANES * t:LANES * t + LANES])
            g = c // LANES + t
            qbd[g, 0:nope, 0:pair] = qt[0:nope, :]
            qbd[g, nope:2 * nope, pair:2 * pair] = qt[nope:2 * nope, :]
    ld_qr.wait()
    qr_all = dot_nn(c_q, wqr[...])
    for t in range(groups // 2):
        qt = jnp.transpose(rotate(qr_all[:, LANES * t:LANES * t + LANES], tabs).astype(BF16))
        for k in range(4):
            lo = (k % 2) * pair
            qbd[2 * t + k // 2, LANES + rope * k:LANES + rope * k + rope, lo:lo + pair] = qt[rope * k:rope * k + rope, :]

    near = me // part
    q_in = lax.rem(iota((1, pair), 1), rows)
    q_dev = 2 * chip + iota((1, pair), 1) // rows
    q_tok = jnp.where(q_in < half, half * q_dev + q_in, half * (2 * n - 1 - q_dev) + q_in - half)
    q_first = q_tok - pos_row
    sides = (near, 1 - near)
    for side in range(2):
        r = iota((keys, pair), 0)
        k_in = lax.rem(r, rows)
        k_dev = part * sides[side] + r // rows
        k_tok = jnp.where(k_in < half, half * k_dev + k_in, half * (2 * n - 1 - k_dev) + k_in - half)
        ok = (k_tok <= q_tok) & (k_tok >= q_first)
        bias[side] = jnp.where(ok, jnp.inf, -jnp.inf)

    spread_r = iota((LANES, 4 * LANES), 0)
    spread_c = iota((LANES, 4 * LANES), 1)
    spread = (spread_r == rope * (spread_c // LANES) + lax.rem(spread_c, rope)).astype(F32).astype(BF16)
    scale2 = (nope + rope) ** -0.5 * math.log2(math.e)
    ld_uk.wait()
    ld_uv.wait()

    def attend(side):
        slots = pl.ds(part * sides[side], part)
        c_all = jnp.concatenate([gath[slots, 0:rows, :].reshape(keys, LANES), gath[slots, rows:2 * rows, :].reshape(keys, LANES)], axis=1)
        wide = dot_nn(gath[slots, 2 * rows:2 * rows + 16, :].reshape(part * 16, LANES), spread).astype(BF16)
        krep = jnp.concatenate([wide[16 * j:16 * j + 16, LANES * b:LANES * b + LANES] for j in range(part) for b in range(rows // 16)], axis=0)
        for c in range(0, cols, 256):
            kn_s[side, :, c:c + 256] = dot_nn(c_all, wuk[:, c:c + 256]).astype(BF16)
            vt_s[side, c:c + 256, :] = dot_tt(wuv[:, c:c + 256], c_all).astype(BF16)
        for g in range(groups):
            lanes = slice(g * LANES, (g + 1) * LANES)
            s = dot_nn(jnp.concatenate([kn_s[side, :, lanes], krep], axis=1), qbd[g])
            limit = bias[side]
            s = jnp.minimum(s, jnp.concatenate([limit, limit], axis=1))
            m = jnp.max(s, axis=0, keepdims=True)
            if side == 1:
                m_old = m_s[g]
                m = jnp.maximum(m, m_old)
            p = jnp.exp2((s - m) * scale2)
            l = jnp.sum(p, axis=0, keepdims=True)
            o = dot_nn(vt_s[side, lanes, :], p.astype(BF16))
            o = [o[:nope, :pair], o[nope:, pair:]]
            if side == 0:
                m_s[g] = m
                l_s[g] = l
                acc_s[g, :nope, :] = o[0]
                acc_s[g, nope:, :] = o[1]
            else:
                alpha = jnp.exp2((m_old - m) * scale2)
                inv = 1.0 / (l_s[g] * alpha + l)
                o = [(acc_s[g, h * nope:(h + 1) * nope, :] * alpha[:, h * pair:(h + 1) * pair] + o[h])
                     * inv[:, h * pair:(h + 1) * pair] for h in range(2)]
                ot = jnp.transpose(jnp.concatenate(o, axis=0).astype(BF16))
                both = [ot[:rows, :], ot[rows:, :]]
                o_own[:, lanes] = jnp.where(core == 0, both[0], both[1])
                o_out[:, lanes] = jnp.where(core == 0, both[1], both[0])

    for c in range(3):
        sends[c].wait()
    attend(0)
    for c in range(3, n - 1):
        sends[c].wait()
    attend(1)

    pair_o = to_partner(o_out, o_in, 2)
    for c in ld_out:
        c.wait()
    ov = o_own[...]
    for c in range(0, y_ref.shape[1], 512):
        y_acc[:, c:c + 512] = dot_nn(ov, wout[:cols, c:c + 512])
    pair_o.wait()
    ov = o_in[...]
    for c in range(0, y_ref.shape[1], 512):
        y_ref[:, c:c + 512] = (y_acc[:, c:c + 512] + dot_nn(ov, wout[cols:, c:c + 512])).astype(BF16)


def solution(mesh):
    n = mesh.shape['ctx']
    row_spec = P(('dp', 'ctx'), None)
    id_spec = P(('dp', 'ctx'))

    def per_device(x_rows, pos_rows, seg_rows, w_dq, w_uq, w_qr, w_dkv, w_kr, w_uk, w_uv, w_out, gain_q, gain_kv):
        rows, d_model = x_rows.shape
        rope = w_kr.shape[1]
        nope = w_uq.shape[1] * rope // w_qr.shape[1]
        cols = w_uq.shape[1] // 2
        groups = cols // LANES
        keys = n // 2 * rows
        operands = (x_rows, pos_rows.reshape(1, rows), w_dq, w_uq, w_qr, w_dkv, w_kr.T, w_uk, w_uv, w_out, gain_q, gain_kv)
        operands = tuple(pltpu.with_memory_space_constraint(a, pltpu.HBM) for a in operands)
        vm = lambda a: pltpu.VMEM(a.shape, a.dtype)
        cut = lambda a: pltpu.VMEM((a.shape[0], a.shape[1] // 2), a.dtype)
        return pl.pallas_call(
            functools.partial(kernel, n, rows, rope, nope),
            out_shape=jax.ShapeDtypeStruct((rows, w_out.shape[1]), BF16),
            in_specs=[pl.BlockSpec(memory_space=pl.ANY)] * len(operands),
            out_specs=pl.BlockSpec(memory_space=pltpu.VMEM),
            scratch_shapes=[
                pltpu.VMEM((2 * rows, d_model), BF16),
                pltpu.VMEM((2, 1, rows), jnp.int32),
                vm(w_dq), cut(w_uq), cut(w_qr), vm(w_dkv), vm(w_kr.T), cut(w_uk), cut(w_uv), vm(w_out), vm(gain_q), vm(gain_kv),
                pltpu.VMEM((2 * rows + 16, LANES), BF16),
                pltpu.VMEM((n, 2 * rows + 16, LANES), BF16),
                pltpu.VMEM((2, keys, 2 * rows), F32),
                pltpu.VMEM((groups, 2 * LANES, 4 * rows), BF16),
                pltpu.VMEM((2, keys, cols), BF16),
                pltpu.VMEM((2, cols, keys), BF16),
                pltpu.VMEM((groups, 1, 4 * rows), F32),
                pltpu.VMEM((groups, 1, 4 * rows), F32),
                pltpu.VMEM((groups, 2 * nope, 2 * rows), F32),
                pltpu.VMEM((rows, cols), BF16),
                pltpu.VMEM((rows, cols), BF16),
                pltpu.VMEM((rows, cols), BF16),
                pltpu.VMEM((rows, w_out.shape[1]), F32),
                pltpu.SemaphoreType.DMA((40,)),
                pltpu.SemaphoreType.DMA((n - 1,)),
                pltpu.SemaphoreType.DMA((n - 1,)),
                pltpu.SemaphoreType.DMA((3,)),
                pltpu.SemaphoreType.DMA((3,)),
            ],
            compiler_params=pltpu.CompilerParams(collective_id=0, has_side_effects=True, vmem_limit_bytes=42 * 1024 * 1024),
        )(*operands)

    return jax.shard_map(per_device, mesh=mesh, in_specs=(row_spec, id_spec, id_spec) + (P(),) * 10, out_specs=row_spec, check_vma=False)
```

time: 20.4 us -> 18.4 us (0.902)
  Pallas kernels: 19.6 us -> 17.6 us
    pallas_call x1, Pallas kernels: 19.6 us -> 17.6 us  [per_device(): pl.pallas_call(functools.partial(kernel, n, rows, rope, nope), out_shape=...]
where the time goes in v3:
time: 18.4 us; the launch traced here: 18.3 us
  Pallas kernels  17.6 us (96%)
  local copies, waits for them, and re-layouts  0.73 us (4%)
    pallas_call x1, Pallas kernels, per_device(): pl.pallas_call(functools.partial(kernel, n, rows, rope, nope), out_shape=...  17.6 us
    unnamed x1, local copies, waits for them, and re-layouts  0.73 us

profile of v3, /device:TPU:0, one launch (start us, length us, event | category | flops | bytes accessed | tf_op | source)
XLA Modules:
  0.0 18.3 jit_solution(4211209759405240501)
XLA Ops:
  0.0 17.6 %shard_map.118 = bf16[64,2560]{1,0:T(8,128)(2,1)S(1)} custom-call(bf16[64,2560]{1,0:T(8,128)(2,1)} %x_hbm.1, s32[1,64]{1,0:T(1,128)} %bitcast.3, bf16[2560,768]{1,0:T(8,128)(2,1)} %wdq_hbm.1, bf16[768,2560]{1,0:T(8,128)(2,1)} %wuq_hbm.1, bf16[768,1280]{1,0:T(8,128)(2,1)} %wqr_hbm.1, bf16[2560,256]{1,0:T(8,128)(2,1)} %wdkv_hbm.1, bf16[32,2560]{1,0:T(8,128)(2,1)} %bitcast.2, ...), custom_call_target="tpu_custom_call" | custom-call | tf_op jit(solution)/shard_map/pallas_call | solution.py:278
  17.6 0.7 %copy.14 = bf16[64,2560]{1,0:T(8,128)(2,1)} copy(bf16[64,2560]{1,0:T(8,128)(2,1)S(1)} %shard_map.118) | data formatting | bytes 655360

commit v4 on v3

--- a/solution.py
+++ b/solution.py
@@ -14,6 +14,8 @@
 F32 = jnp.float32
 BF16 = jnp.bfloat16
 LANES = 128
+AHEAD = 2
+SLOTS = AHEAD + 1
 
 
 def rms_rows(vals, gain):
@@ -39,7 +41,7 @@
 
 def kernel(n, rows, rope, nope, x_hbm, pos_hbm, wdq_hbm, wuq_hbm, wqr_hbm, wdkv_hbm, wkr_hbm, wuk_hbm, wuv_hbm, wout_hbm,
            gq_hbm, gkv_hbm, y_ref, x, pos, wdq, wuq, wqr, wdkv, wkr, wuk, wuv, wout, gq, gkv,
-           lat, gath, bias, qbd, kn_s, vt_s, m_s, l_s, acc_s, o_own, o_out, o_in, y_acc,
+           lat, gath, bias, qbd, kn_s, vt_s, m_s, l_s, acc_s, o_own, o_out, o_in, y_acc, s_s,
            load_sem, send_sem, recv_sem, pair_send, pair_recv):
     me = lax.axis_index('ctx')
     core = lax.rem(me, 2)
@@ -209,19 +211,21 @@
         c_all = jnp.concatenate([gath[slots, 0:rows, :].reshape(keys, LANES), gath[slots, rows:2 * rows, :].reshape(keys, LANES)], axis=1)
         wide = dot_nn(gath[slots, 2 * rows:2 * rows + 16, :].reshape(part * 16, LANES), spread).astype(BF16)
         krep = jnp.concatenate([wide[16 * j:16 * j + 16, LANES * b:LANES * b + LANES] for j in range(part) for b in range(rows // 16)], axis=0)
-        for c in range(0, cols, 256):
+        def project(c):
             kn_s[side, :, c:c + 256] = dot_nn(c_all, wuk[:, c:c + 256]).astype(BF16)
             vt_s[side, c:c + 256, :] = dot_tt(wuv[:, c:c + 256], c_all).astype(BF16)
-        for g in range(groups):
-            lanes = slice(g * LANES, (g + 1) * LANES)
-            s = dot_nn(jnp.concatenate([kn_s[side, :, lanes], krep], axis=1), qbd[g])
+
+        def score(g):
+            s = dot_nn(jnp.concatenate([kn_s[side, :, g * LANES:(g + 1) * LANES], krep], axis=1), qbd[g])
             limit = bias[side]
             s = jnp.minimum(s, jnp.concatenate([limit, limit], axis=1))
+            s_s[g % SLOTS] = s
             m = jnp.max(s, axis=0, keepdims=True)
-            if side == 1:
-                m_old = m_s[g]
-                m = jnp.maximum(m, m_old)
-            p = jnp.exp2((s - m) * scale2)
+            return m if side == 0 else jnp.maximum(m, m_s[g])
+
+        def finish(g, m):
+            lanes = slice(g * LANES, (g + 1) * LANES)
+            p = jnp.exp2((s_s[g % SLOTS] - m) * scale2)
             l = jnp.sum(p, axis=0, keepdims=True)
             o = dot_nn(vt_s[side, lanes, :], p.astype(BF16))
             o = [o[:nope, :pair], o[nope:, pair:]]
@@ -231,7 +235,7 @@
                 acc_s[g, :nope, :] = o[0]
                 acc_s[g, nope:, :] = o[1]
             else:
-                alpha = jnp.exp2((m_old - m) * scale2)
+                alpha = jnp.exp2((m_s[g] - m) * scale2)
                 inv = 1.0 / (l_s[g] * alpha + l)
                 o = [(acc_s[g, h * nope:(h + 1) * nope, :] * alpha[:, h * pair:(h + 1) * pair] + o[h])
                      * inv[:, h * pair:(h + 1) * pair] for h in range(2)]
@@ -239,6 +243,17 @@
                 both = [ot[:rows, :], ot[rows:, :]]
                 o_own[:, lanes] = jnp.where(core == 0, both[0], both[1])
                 o_out[:, lanes] = jnp.where(core == 0, both[1], both[0])
+
+        tops = {}
+        project(0)
+        for g in range(AHEAD):
+            tops[g] = score(g)
+        for g in range(groups):
+            if g % 2 == 0 and (g + 2) * LANES < cols:
+                project((g + 2) * LANES)
+            if g + AHEAD < groups:
+                tops[g + AHEAD] = score(g + AHEAD)
+            finish(g, tops[g])
 
     for c in range(3):
         sends[c].wait()
@@ -297,6 +312,7 @@
                 pltpu.VMEM((rows, cols), BF16),
                 pltpu.VMEM((rows, cols), BF16),
                 pltpu.VMEM((rows, w_out.shape[1]), F32),
+                pltpu.VMEM((SLOTS, keys, 4 * rows), F32),
                 pltpu.SemaphoreType.DMA((40,)),
                 pltpu.SemaphoreType.DMA((n - 1,)),
                 pltpu.SemaphoreType.DMA((n - 1,)),

time: 18.4 us -> 15.5 us (0.84)
  Pallas kernels: 17.6 us -> 14.7 us
    pallas_call x1, Pallas kernels: 17.6 us -> 14.7 us  [per_device(): pl.pallas_call(functools.partial(kernel, n, rows, rope, nope), out_shape=...]
where the time goes in v4:
time: 15.5 us; the launch traced here: 15.4 us
  Pallas kernels  14.7 us (95%)
  local copies, waits for them, and re-layouts  0.73 us (5%)
    pallas_call x1, Pallas kernels, per_device(): pl.pallas_call(functools.partial(kernel, n, rows, rope, nope), out_shape=...  14.7 us
    unnamed x1, local copies, waits for them, and re-layouts  0.73 us

profile of v4, /device:TPU:0, one launch (start us, length us, event | category | flops | bytes accessed | tf_op | source)
XLA Modules:
  0.0 15.4 jit_solution(16313222641008884198)
XLA Ops:
  0.0 14.7 %shard_map.118 = bf16[64,2560]{1,0:T(8,128)(2,1)S(1)} custom-call(bf16[64,2560]{1,0:T(8,128)(2,1)} %x_hbm.1, s32[1,64]{1,0:T(1,128)} %bitcast.3, bf16[2560,768]{1,0:T(8,128)(2,1)} %wdq_hbm.1, bf16[768,2560]{1,0:T(8,128)(2,1)} %wuq_hbm.1, bf16[768,1280]{1,0:T(8,128)(2,1)} %wqr_hbm.1, bf16[2560,256]{1,0:T(8,128)(2,1)} %wdkv_hbm.1, bf16[32,2560]{1,0:T(8,128)(2,1)} %bitcast.2, ...), custom_call_target="tpu_custom_call" | custom-call | tf_op jit(solution)/shard_map/pallas_call | solution.py:293
  14.7 0.7 %copy.14 = bf16[64,2560]{1,0:T(8,128)(2,1)} copy(bf16[64,2560]{1,0:T(8,128)(2,1)S(1)} %shard_map.118) | data formatting | bytes 655360

commit v5 on v3

v5 whole, which is shorter than its diff:
```python
import functools
import math

import numpy as np
import jax
import jax.numpy as jnp
from jax import lax
from jax.experimental import pallas as pl
from jax.experimental.pallas import tpu as pltpu
from jax.sharding import PartitionSpec as P

NORM_EPS = 1e-6
MESH = pl.DeviceIdType.MESH
F32 = jnp.float32
BF16 = jnp.bfloat16
LANES = 128
STAGES = (2, 3, 4)
LEAD = 2
SLOTS = 5
OUT_COLS = 512
STRIP = 32


def rms_rows(vals, gain):
    mean_sq = jnp.mean(vals * vals, axis=-1, keepdims=True)
    return (vals * lax.rsqrt(mean_sq + NORM_EPS) * gain.astype(F32)).astype(BF16)


def dot_nn(a, b):
    return lax.dot_general(a, b, (((1,), (0,)), ((), ())), preferred_element_type=F32)


def dot_nt(a, b):
    return lax.dot_general(a, b, (((1,), (1,)), ((), ())), preferred_element_type=F32)


def dot_tt(a, b):
    return lax.dot_general(a, b, (((0,), (1,)), ((), ())), preferred_element_type=F32)


def iota(shape, axis):
    return lax.broadcasted_iota(jnp.int32, shape, axis)


def kernel(n, rows, rope, nope, x_hbm, pos_hbm, wdq_hbm, wuq_hbm, wqr_hbm, wdkv_hbm, wkr_hbm, wuk_hbm, wuv_hbm, wout_hbm,
           gq_hbm, gkv_hbm, y_ref, x, pos, wdq, wuq, wqr, wdkv, wkr, wukv, wout, gq, gkv,
           cq, lat, gath, bias, qbd, kn_s, vt_s, m_s, l_s, acc_s, o_own, o_out, o_in, y_acc, s_s, p_s,
           load_sem, send_sem, recv_sem, pair_send, pair_recv):
    me = lax.axis_index('ctx')
    core = lax.rem(me, 2)
    chip = me // 2
    partner = me + 1 - 2 * core
    half = rows // 2
    rank = wdkv.shape[1]
    pair = 2 * rows
    cols = wuq.shape[1]
    groups = cols // LANES
    tables = rope // 2

    barrier = pltpu.get_barrier_semaphore()
    for j in range(1, n):
        pl.semaphore_signal(barrier, inc=1, device_id={'ctx': lax.rem(me + j, n)}, device_id_type=MESH)

    loads = []

    def load(src, dst, sem=None):
        sem = len(loads) if sem is None else sem
        copy = pltpu.make_async_copy(src, dst, load_sem.at[sem])
        copy.start()
        loads.append(copy)
        return copy

    def wait_all(ref, sem):
        pltpu.make_async_copy(ref, ref, sem).wait()

    mine = pl.ds(pl.multiple_of(core * rows, rows), rows)
    head_cols = pl.ds(pl.multiple_of(core * cols, LANES), cols)
    rope_cols = pl.ds(pl.multiple_of(core * wqr.shape[1], LANES), wqr.shape[1])
    d_model = x.shape[1]
    cuts = [(0, 1024), (1024, 1024), (2048, d_model - 2048)]
    ld_x = load(x_hbm, x.at[pl.ds(0, rows), :])
    x[rows:, :] = jnp.zeros((rows, d_model), BF16)
    o_own[rows:, :] = jnp.zeros((rows, cols), BF16)
    o_in[rows:, :] = jnp.zeros((rows, cols), BF16)
    ld_kr = load(wkr_hbm, wkr)
    ld_pos = load(pos_hbm, pos.at[core])
    ld_dkv = [load(wdkv_hbm.at[pl.ds(c, h), :], wdkv.at[pl.ds(c, h), :]) for c, h in cuts]
    ld_gkv = load(gkv_hbm, gkv)
    ld_dq = load(wdq_hbm, wdq)
    ld_gq = load(gq_hbm, gq)
    ld_uq = load(wuq_hbm.at[:, head_cols], wuq)
    ld_qr = load(wqr_hbm.at[:, rope_cols], wqr)
    ukv = len(loads)
    load(wuk_hbm.at[:, head_cols], wukv.at[0], ukv)
    load(wuv_hbm.at[:, head_cols], wukv.at[1], ukv)
    row_a = pl.multiple_of(core * cols, LANES)
    row_b = pl.multiple_of((1 - core) * cols, LANES)
    ld_out = [load(wout_hbm.at[pl.ds(row, cols), :], wout.at[pl.ds(at, cols), :], ukv + 1 + i) for i, (row, at) in enumerate(((row_a, 0), (row_b, cols)))]

    def rope_tables(pos_row):
        width = pos_row.shape[1]
        freq = iota((tables, width), 0)
        inv_freq = jnp.zeros((tables, width), F32)
        for i in range(tables):
            inv_freq = jnp.where(freq == i, np.float32(10000.0 ** (-2.0 * i / rope)), inv_freq)
        angles = pos_row.astype(F32) * inv_freq

        def table(vals):
            tall = jnp.concatenate([vals] * (LANES // tables), axis=0)
            if width < LANES:
                tall = jnp.concatenate([tall] * (LANES // width), axis=1)
            return jnp.transpose(tall)[:width, :]

        lead = lax.rem(iota((width, LANES), 1), rope) < tables
        cos_t, sin_t = table(jnp.cos(angles)), table(jnp.sin(angles))
        return cos_t, jnp.where(lead, -sin_t, sin_t), lead

    def rotate(a, tabs):
        cos_t, sin_t, lead = tabs
        other = jnp.where(lead, pltpu.roll(a, LANES - tables, 1), pltpu.roll(a, tables, 1))
        return a * cos_t + other * sin_t

    ld_pos.wait()
    tabs = rope_tables(pos[core])
    ld_x.wait()
    ld_kr.wait()
    kr = dot_nt(x[0:rows, :], wkr[...])
    c_kv = None
    for c, (first, height) in zip(ld_dkv, cuts):
        c.wait()
        term = dot_nn(x[0:rows, first:first + height], wdkv[first:first + height, :])
        c_kv = term if c_kv is None else c_kv + term
    ld_gkv.wait()
    c_kv = rms_rows(c_kv, gkv[...].reshape(1, rank))
    kr = rotate(jnp.concatenate([kr] * (LANES // rope), axis=1), tabs)
    pack = kr[0:16, :]
    lane16 = iota((16, LANES), 1) // rope
    for b in range(1, rows // 16):
        pack = jnp.where(lane16 == b, kr[16 * b:16 * b + 16, :], pack)
    pack = pack.astype(BF16)
    lat[0:rows, :] = c_kv[:, :LANES]
    lat[rows:2 * rows, :] = c_kv[:, LANES:]
    lat[2 * rows:2 * rows + 16, :] = pack
    gath[me, 0:rows, :] = c_kv[:, :LANES]
    gath[me, rows:2 * rows, :] = c_kv[:, LANES:]
    gath[me, 2 * rows:2 * rows + 16, :] = pack

    def query_latents():
        ld_dq.wait()
        ld_gq.wait()
        both = dot_nn(x[...], wdq[...])
        cq[mine, :] = rms_rows(both[:rows, :] + both[rows:, :], gq[...].reshape(1, wdq.shape[1]))

    pl.when(chip == 0)(query_latents)
    pl.semaphore_wait(barrier, n - 1)
    bit0, bit1 = lax.rem(chip, 2), chip // 2
    for j in range(1, n):
        flip_chip, flip_core = j // 2, j % 2
        peer_chip = (bit0 + (flip_chip % 2) * (1 - 2 * bit0)) + 2 * (bit1 + (flip_chip // 2) * (1 - 2 * bit1))
        peer = 2 * peer_chip + core + flip_core * (1 - 2 * core)
        pltpu.make_async_remote_copy(
            src_ref=lat, dst_ref=gath.at[me], send_sem=send_sem.at[0], recv_sem=recv_sem.at[(flip_chip + 1) // 2],
            device_id={'ctx': peer}, device_id_type=MESH).start()

    def to_partner(src, dst, index):
        copy = pltpu.make_async_remote_copy(
            src_ref=src, dst_ref=dst, send_sem=pair_send.at[index], recv_sem=pair_recv.at[index],
            device_id={'ctx': partner}, device_id_type=MESH)
        copy.start()
        return copy

    pair_pos = to_partner(pos.at[core], pos.at[core], 0)

    pl.when(chip > 0)(query_latents)
    pair_cq = to_partner(cq.at[mine, :], cq.at[mine, :], 1)
    qbd[...] = jnp.zeros_like(qbd)
    pair_pos.wait()
    pos_row = jnp.concatenate([pos[0], pos[1]], axis=1)
    tabs = rope_tables(pos_row)

    q_in = lax.rem(iota((1, pair), 1), rows)
    q_dev = 2 * chip + iota((1, pair), 1) // rows
    q_tok = jnp.where(q_in < half, half * q_dev + q_in, half * (2 * n - 1 - q_dev) + q_in - half)
    q_first = q_tok - pos_row
    side0, side1 = 1 - 2 * bit0, 2 - 4 * bit1
    chips = (chip, chip + side0, chip + side1, chip + side0 + side1)
    chunks = (chips[:1], chips[1:3], chips[3:])
    for i, owner in enumerate(chips):
        r = iota((pair, pair), 0)
        k_in = lax.rem(r, rows)
        k_dev = 2 * owner + r // rows
        k_tok = jnp.where(k_in < half, half * k_dev + k_in, half * (2 * n - 1 - k_dev) + k_in - half)
        ok = (k_tok <= q_tok) & (k_tok >= q_first)
        bias[i * pair:(i + 1) * pair, :] = jnp.where(ok, jnp.inf, -jnp.inf)

    pair_cq.wait()
    c_q = cq[...]
    ld_uq.wait()
    ld_qr.wait()
    qr_all = dot_nn(c_q, wqr[...])
    q_cols = {c: dot_nn(c_q, wuq[:, c:c + 256]).astype(BF16) for c in range(0, cols, 256)}
    for t in range(groups // 2):
        qt = jnp.transpose(rotate(qr_all[:, LANES * t:LANES * t + LANES], tabs).astype(BF16))
        for k in range(4):
            lo = (k % 2) * pair
            qbd[2 * t + k // 2, LANES + rope * k:LANES + rope * k + rope, lo:lo + pair] = qt[rope * k:rope * k + rope, :]
    for g in range(groups):
        qt = jnp.transpose(q_cols[g // 2 * 256][:, g % 2 * LANES:g % 2 * LANES + LANES])
        qbd[g, 0:nope, 0:pair] = qt[0:nope, :]
        qbd[g, nope:2 * nope, pair:2 * pair] = qt[nope:2 * nope, :]

    spread_r = iota((LANES, 4 * LANES), 0)
    spread_c = iota((LANES, 4 * LANES), 1)
    spread = (spread_r == rope * (spread_c // LANES) + lax.rem(spread_c, rope)).astype(F32).astype(BF16)
    scale2 = (nope + rope) ** -0.5 * math.log2(math.e)
    wait_all(wukv, load_sem.at[ukv])

    def attend(index):
        owners = chunks[index]
        count = 2 * len(owners)
        keys = count * rows
        base = 2 * sum(len(c) for c in chunks[:index])

        def rows_of(first, size):
            parts = [gath[pl.ds(2 * owner, 2), first:first + size, :].reshape(2 * size, LANES) for owner in owners]
            return jnp.concatenate(parts, axis=0)

        c_all = jnp.concatenate([rows_of(0, rows), rows_of(rows, rows)], axis=1)
        wide = dot_nn(rows_of(2 * rows, 16), spread).astype(BF16)
        krep = jnp.concatenate([wide[16 * j:16 * j + 16, LANES * b:LANES * b + LANES] for j in range(count) for b in range(rows // 16)], axis=0)

        def project(c):
            kn_s[0:keys, c:c + 256] = dot_nn(c_all, wukv[0, :, c:c + 256]).astype(BF16)
            vt_s[c:c + 256, 0:keys] = dot_tt(wukv[1, :, c:c + 256], c_all).astype(BF16)

        def score(g):
            s = dot_nn(jnp.concatenate([kn_s[0:keys, g * LANES:(g + 1) * LANES], krep], axis=1), qbd[g])
            tall = None
            for r in range(0, keys, STRIP):
                limit = bias[base * rows + r:base * rows + r + STRIP, :]
                strip = jnp.minimum(s[r:r + STRIP, :], jnp.concatenate([limit, limit], axis=1))
                s_s[g % SLOTS, r:r + STRIP, :] = strip
                for k in range(0, STRIP, 8):
                    tall = strip[k:k + 8, :] if tall is None else jnp.maximum(tall, strip[k:k + 8, :])
            m = jnp.max(tall, axis=0, keepdims=True)
            tops[g] = m if index == 0 else jnp.maximum(m, m_s[g])

        def weigh(g):
            total = None
            for r in range(0, keys, STRIP):
                p = jnp.exp2((s_s[g % SLOTS, r:r + STRIP, :] - tops[g]) * scale2)
                p_s[g % SLOTS, r:r + STRIP, :] = p.astype(BF16)
                for k in range(0, STRIP, 8):
                    total = p[k:k + 8, :] if total is None else total + p[k:k + 8, :]
            sums[g] = jnp.sum(total, axis=0, keepdims=True)

        def mix(g):
            o = dot_nn(vt_s[g * LANES:(g + 1) * LANES, 0:keys], p_s[g % SLOTS, 0:keys, :])
            outs[g] = [o[:nope, :pair], o[nope:, pair:]]

        def finish(g):
            lanes = slice(g * LANES, (g + 1) * LANES)
            m, l, o = tops[g], sums[g], outs[g]
            if index > 0:
                alpha = jnp.exp2((m_s[g] - m) * scale2)
                l = l_s[g] * alpha + l
                o = [acc_s[g, h * nope:(h + 1) * nope, :] * alpha[:, h * pair:(h + 1) * pair] + o[h] for h in range(2)]
            if index < len(chunks) - 1:
                m_s[g] = m
                l_s[g] = l
                acc_s[g, :nope, :] = o[0]
                acc_s[g, nope:, :] = o[1]
            else:
                inv = 1.0 / l
                o = [o[h] * inv[:, h * pair:(h + 1) * pair] for h in range(2)]
                ot = jnp.transpose(jnp.concatenate(o, axis=0).astype(BF16))
                both = [ot[:rows, :], ot[rows:, :]]
                o_own[0:rows, lanes] = jnp.where(core == 0, both[0], both[1])
                o_out[:, lanes] = jnp.where(core == 0, both[1], both[0])

        tops, sums, outs = {}, {}, {}
        project(0)
        for t in range(groups + STAGES[2]):
            if t % 2 == 0 and 0 < t + LEAD < groups:
                project((t + LEAD) * LANES)
            for stage, lag in ((score, 0), (weigh, STAGES[0]), (mix, STAGES[1]), (finish, STAGES[2])):
                if 0 <= t - lag < groups:
                    stage(t - lag)

    wait_all(gath.at[pl.ds(0, 1)], recv_sem.at[0])
    attend(0)
    wait_all(gath.at[pl.ds(0, 4)], recv_sem.at[1])
    attend(1)
    wait_all(gath.at[pl.ds(0, 2)], recv_sem.at[2])
    attend(2)

    pair_o = to_partner(o_out, o_in.at[pl.ds(0, rows), :], 2)
    wait_all(gath.at[pl.ds(0, n - 1)], send_sem.at[0])
    for c in ld_out:
        c.wait()
    ov = o_own[...]
    for c in range(0, d_model, OUT_COLS):
        y_acc[:, c:c + OUT_COLS] = dot_nn(ov, wout[:cols, c:c + OUT_COLS])
    pair_o.wait()
    ov = o_in[...]
    for c in range(0, d_model, OUT_COLS):
        out = y_acc[:, c:c + OUT_COLS] + dot_nn(ov, wout[cols:, c:c + OUT_COLS])
        y_ref[:, c:c + OUT_COLS] = (out[:rows, :] + out[rows:, :]).astype(BF16)


def solution(mesh):
    n = mesh.shape['ctx']
    row_spec = P(('dp', 'ctx'), None)
    id_spec = P(('dp', 'ctx'))

    def per_device(x_rows, pos_rows, seg_rows, w_dq, w_uq, w_qr, w_dkv, w_kr, w_uk, w_uv, w_out, gain_q, gain_kv):
        rows, d_model = x_rows.shape
        rope = w_kr.shape[1]
        nope = w_uq.shape[1] * rope // w_qr.shape[1]
        cols = w_uq.shape[1] // 2
        groups = cols // LANES
        keys = n // 2 * rows
        operands = (x_rows, pos_rows.reshape(1, rows), w_dq, w_uq, w_qr, w_dkv, w_kr.T, w_uk, w_uv, w_out, gain_q, gain_kv)
        operands = tuple(pltpu.with_memory_space_constraint(a, pltpu.HBM) for a in operands)
        vm = lambda a: pltpu.VMEM(a.shape, a.dtype)
        cut = lambda a: pltpu.VMEM((a.shape[0], a.shape[1] // 2), a.dtype)
        return pl.pallas_call(
            functools.partial(kernel, n, rows, rope, nope),
            out_shape=jax.ShapeDtypeStruct((rows, w_out.shape[1]), BF16),
            in_specs=[pl.BlockSpec(memory_space=pl.ANY)] * len(operands),
            out_specs=pl.BlockSpec(memory_space=pltpu.VMEM),
            scratch_shapes=[
                pltpu.VMEM((2 * rows, d_model), BF16),
                pltpu.VMEM((2, 1, rows), jnp.int32),
                vm(w_dq), cut(w_uq), cut(w_qr), vm(w_dkv), vm(w_kr.T),
                pltpu.VMEM((2, w_uk.shape[0], cols), BF16),
                vm(w_out), vm(gain_q), vm(gain_kv),
                pltpu.VMEM((2 * rows, w_dq.shape[1]), BF16),
                pltpu.VMEM((2 * rows + 16, LANES), BF16),
                pltpu.VMEM((n, 2 * rows + 16, LANES), BF16),
                pltpu.VMEM((n * rows, 2 * rows), F32),
                pltpu.VMEM((groups, 2 * LANES, 4 * rows), BF16),
                pltpu.VMEM((keys, cols), BF16),
                pltpu.VMEM((cols, keys), BF16),
                pltpu.VMEM((groups, 1, 4 * rows), F32),
                pltpu.VMEM((groups, 1, 4 * rows), F32),
                pltpu.VMEM((groups, 2 * nope, 2 * rows), F32),
                pltpu.VMEM((2 * rows, cols), BF16),
                pltpu.VMEM((rows, cols), BF16),
                pltpu.VMEM((2 * rows, cols), BF16),
                pltpu.VMEM((2 * rows, w_out.shape[1]), F32),
                pltpu.VMEM((SLOTS, keys, 4 * rows), F32),
                pltpu.VMEM((SLOTS, keys, 4 * rows), BF16),
                pltpu.SemaphoreType.DMA((14,)),
                pltpu.SemaphoreType.DMA((1,)),
                pltpu.SemaphoreType.DMA((3,)),
                pltpu.SemaphoreType.DMA((3,)),
                pltpu.SemaphoreType.DMA((3,)),
            ],
            compiler_params=pltpu.CompilerParams(collective_id=0, has_side_effects=True, vmem_limit_bytes=42 * 1024 * 1024),
        )(*operands)

    return jax.shard_map(per_device, mesh=mesh, in_specs=(row_spec, id_spec, id_spec) + (P(),) * 10, out_specs=row_spec, check_vma=False)
```

time: 18.4 us -> 14 us (0.76)
  Pallas kernels: 17.6 us -> 13.2 us
    pallas_call x1, Pallas kernels: 17.6 us -> 13.2 us  [per_device(): pl.pallas_call(functools.partial(kernel, n, rows, rope, nope), out_shape=...]
where the time goes in v5:
time: 14 us
  Pallas kernels  13.2 us (94%)
  local copies, waits for them, and re-layouts  0.73 us (5%)
    pallas_call x1, Pallas kernels, per_device(): pl.pallas_call(functools.partial(kernel, n, rows, rope, nope), out_shape=...  13.2 us
    unnamed x1, local copies, waits for them, and re-layouts  0.73 us

profile of v5, /device:TPU:0, one launch (start us, length us, event | category | flops | bytes accessed | tf_op | source)
XLA Modules:
  0.0 14.0 jit_solution(4559760344316026495)
XLA Ops:
  0.0 13.2 %shard_map.118 = bf16[64,2560]{1,0:T(8,128)(2,1)S(1)} custom-call(bf16[64,2560]{1,0:T(8,128)(2,1)} %x_hbm.1, s32[1,64]{1,0:T(1,128)} %bitcast.3, bf16[2560,768]{1,0:T(8,128)(2,1)} %wdq_hbm.1, bf16[768,2560]{1,0:T(8,128)(2,1)} %wuq_hbm.1, bf16[768,1280]{1,0:T(8,128)(2,1)} %wqr_hbm.1, bf16[2560,256]{1,0:T(8,128)(2,1)} %wdkv_hbm.1, bf16[32,2560]{1,0:T(8,128)(2,1)} %bitcast.2, ...), custom_call_target="tpu_custom_call" | custom-call | tf_op jit(solution)/shard_map/pallas_call | solution.py:327
  13.2 0.7 %copy.14 = bf16[64,2560]{1,0:T(8,128)(2,1)} copy(bf16[64,2560]{1,0:T(8,128)(2,1)S(1)} %shard_map.118) | data formatting | bytes 655360

commit v6 on v5

--- a/solution.py
+++ b/solution.py
@@ -14,9 +14,9 @@
 F32 = jnp.float32
 BF16 = jnp.bfloat16
 LANES = 128
-STAGES = (2, 3, 4)
+STAGES = ((4, 6, 8), (2, 4, 6))
 LEAD = 2
-SLOTS = 5
+SLOTS = 10
 OUT_COLS = 512
 STRIP = 32
 
@@ -78,14 +78,14 @@
     rope_cols = pl.ds(pl.multiple_of(core * wqr.shape[1], LANES), wqr.shape[1])
     d_model = x.shape[1]
     cuts = [(0, 1024), (1024, 1024), (2048, d_model - 2048)]
+    ld_pos = load(pos_hbm, pos.at[core])
     ld_x = load(x_hbm, x.at[pl.ds(0, rows), :])
     x[rows:, :] = jnp.zeros((rows, d_model), BF16)
     o_own[rows:, :] = jnp.zeros((rows, cols), BF16)
     o_in[rows:, :] = jnp.zeros((rows, cols), BF16)
     ld_kr = load(wkr_hbm, wkr)
-    ld_pos = load(pos_hbm, pos.at[core])
+    ld_gkv = load(gkv_hbm, gkv)
     ld_dkv = [load(wdkv_hbm.at[pl.ds(c, h), :], wdkv.at[pl.ds(c, h), :]) for c, h in cuts]
-    ld_gkv = load(gkv_hbm, gkv)
     ld_dq = load(wdq_hbm, wdq)
     ld_gq = load(gq_hbm, gq)
     ld_uq = load(wuq_hbm.at[:, head_cols], wuq)
@@ -279,11 +279,12 @@
                 o_out[:, lanes] = jnp.where(core == 0, both[1], both[0])
 
         tops, sums, outs = {}, {}, {}
+        lags = STAGES[len(owners) - 1]
         project(0)
-        for t in range(groups + STAGES[2]):
+        for t in range(groups + lags[2]):
             if t % 2 == 0 and 0 < t + LEAD < groups:
                 project((t + LEAD) * LANES)
-            for stage, lag in ((score, 0), (weigh, STAGES[0]), (mix, STAGES[1]), (finish, STAGES[2])):
+            for stage, lag in ((score, 0), (weigh, lags[0]), (mix, lags[1]), (finish, lags[2])):
                 if 0 <= t - lag < groups:
                     stage(t - lag)
 

time: 14 us -> 13.9 us (level)
  no operation moved by 1% of the time
where the time goes in v6:
time: 13.9 us; the launch traced here: 13.8 us
  Pallas kernels  13.1 us (94%)
  local copies, waits for them, and re-layouts  0.73 us (5%)
    pallas_call x1, Pallas kernels, per_device(): pl.pallas_call(functools.partial(kernel, n, rows, rope, nope), out_shape=...  13.1 us
    unnamed x1, local copies, waits for them, and re-layouts  0.73 us

profile of v6, /device:TPU:0, one launch (start us, length us, event | category | flops | bytes accessed | tf_op | source)
XLA Modules:
  0.0 13.8 jit_solution(14135611787352540250)
XLA Ops:
  0.0 13.1 %shard_map.118 = bf16[64,2560]{1,0:T(8,128)(2,1)S(1)} custom-call(bf16[64,2560]{1,0:T(8,128)(2,1)} %x_hbm.1, s32[1,64]{1,0:T(1,128)} %bitcast.3, bf16[2560,768]{1,0:T(8,128)(2,1)} %wdq_hbm.1, bf16[768,2560]{1,0:T(8,128)(2,1)} %wuq_hbm.1, bf16[768,1280]{1,0:T(8,128)(2,1)} %wqr_hbm.1, bf16[2560,256]{1,0:T(8,128)(2,1)} %wdkv_hbm.1, bf16[32,2560]{1,0:T(8,128)(2,1)} %bitcast.2, ...), custom_call_target="tpu_custom_call" | custom-call | tf_op jit(solution)/shard_map/pallas_call | solution.py:328
  13.1 0.7 %copy.14 = bf16[64,2560]{1,0:T(8,128)(2,1)} copy(bf16[64,2560]{1,0:T(8,128)(2,1)S(1)} %shard_map.118) | data formatting | bytes 655360

commit v7 on v6

--- a/solution.py
+++ b/solution.py
@@ -17,6 +17,7 @@
 STAGES = ((4, 6, 8), (2, 4, 6))
 LEAD = 2
 SLOTS = 10
+FIRST_SEND = 6
 OUT_COLS = 512
 STRIP = 32
 
@@ -95,7 +96,8 @@
     load(wuv_hbm.at[:, head_cols], wukv.at[1], ukv)
     row_a = pl.multiple_of(core * cols, LANES)
     row_b = pl.multiple_of((1 - core) * cols, LANES)
-    ld_out = [load(wout_hbm.at[pl.ds(row, cols), :], wout.at[pl.ds(at, cols), :], ukv + 1 + i) for i, (row, at) in enumerate(((row_a, 0), (row_b, cols)))]
+    for row, at in ((row_a, 0), (row_b, cols)):
+        load(wout_hbm.at[pl.ds(row, cols), :], wout.at[pl.ds(at, cols), :], ukv + 1)
 
     def rope_tables(pos_row):
         width = pos_row.shape[1]
@@ -154,13 +156,19 @@
     pl.when(chip == 0)(query_latents)
     pl.semaphore_wait(barrier, n - 1)
     bit0, bit1 = lax.rem(chip, 2), chip // 2
-    for j in range(1, n):
-        flip_chip, flip_core = j // 2, j % 2
-        peer_chip = (bit0 + (flip_chip % 2) * (1 - 2 * bit0)) + 2 * (bit1 + (flip_chip // 2) * (1 - 2 * bit1))
+    def send(flip_core, flip_chip, sem):
+        flip0, flip1 = lax.rem(flip_chip, 2), flip_chip // 2
+        peer_chip = (bit0 + flip0 * (1 - 2 * bit0)) + 2 * (bit1 + flip1 * (1 - 2 * bit1))
         peer = 2 * peer_chip + core + flip_core * (1 - 2 * core)
         pltpu.make_async_remote_copy(
-            src_ref=lat, dst_ref=gath.at[me], send_sem=send_sem.at[0], recv_sem=recv_sem.at[(flip_chip + 1) // 2],
+            src_ref=lat, dst_ref=gath.at[me], send_sem=send_sem.at[0], recv_sem=recv_sem.at[sem],
             device_id={'ctx': peer}, device_id_type=MESH).start()
+
+    send(1, 0, 0)
+    for k in range(3):
+        flip_chip = lax.rem(k + 2 * (chip // 3), 3) + 1
+        for flip_core in range(2):
+            send(flip_core, flip_chip, (flip_chip + 2) // 2)
 
     def to_partner(src, dst, index):
         copy = pltpu.make_async_remote_copy(
@@ -184,7 +192,7 @@
     q_first = q_tok - pos_row
     side0, side1 = 1 - 2 * bit0, 2 - 4 * bit1
     chips = (chip, chip + side0, chip + side1, chip + side0 + side1)
-    chunks = (chips[:1], chips[1:3], chips[3:])
+    chunks = (chips[:1], chips[1:2], chips[2:])
     for i, owner in enumerate(chips):
         r = iota((pair, pair), 0)
         k_in = lax.rem(r, rows)
@@ -214,6 +222,12 @@
     spread = (spread_r == rope * (spread_c // LANES) + lax.rem(spread_c, rope)).astype(F32).astype(BF16)
     scale2 = (nope + rope) ** -0.5 * math.log2(math.e)
     wait_all(wukv, load_sem.at[ukv])
+
+    pair_o = []
+
+    def send_heads(first, last, index):
+        part = pl.ds(first * LANES, (last - first) * LANES)
+        return to_partner(o_out.at[:, part], o_in.at[pl.ds(0, rows), part], index)
 
     def attend(index):
         owners = chunks[index]
@@ -277,6 +291,8 @@
                 both = [ot[:rows, :], ot[rows:, :]]
                 o_own[0:rows, lanes] = jnp.where(core == 0, both[0], both[1])
                 o_out[:, lanes] = jnp.where(core == 0, both[1], both[0])
+                if g == FIRST_SEND - 1:
+                    pair_o.append(send_heads(0, FIRST_SEND, 2))
 
         tops, sums, outs = {}, {}, {}
         lags = STAGES[len(owners) - 1]
@@ -290,22 +306,26 @@
 
     wait_all(gath.at[pl.ds(0, 1)], recv_sem.at[0])
     attend(0)
-    wait_all(gath.at[pl.ds(0, 4)], recv_sem.at[1])
+    wait_all(gath.at[pl.ds(0, 2)], recv_sem.at[1])
     attend(1)
-    wait_all(gath.at[pl.ds(0, 2)], recv_sem.at[2])
+    wait_all(gath.at[pl.ds(0, 4)], recv_sem.at[2])
     attend(2)
 
-    pair_o = to_partner(o_out, o_in.at[pl.ds(0, rows), :], 2)
+    pair_o.append(send_heads(FIRST_SEND, groups, 3))
     wait_all(gath.at[pl.ds(0, n - 1)], send_sem.at[0])
-    for c in ld_out:
-        c.wait()
+    wait_all(wout, load_sem.at[ukv + 1])
     ov = o_own[...]
     for c in range(0, d_model, OUT_COLS):
         y_acc[:, c:c + OUT_COLS] = dot_nn(ov, wout[:cols, c:c + OUT_COLS])
-    pair_o.wait()
-    ov = o_in[...]
+    split = FIRST_SEND * LANES
+    pair_o[0].wait()
+    ov = o_in[:, :split]
     for c in range(0, d_model, OUT_COLS):
-        out = y_acc[:, c:c + OUT_COLS] + dot_nn(ov, wout[cols:, c:c + OUT_COLS])
+        y_acc[:, c:c + OUT_COLS] += dot_nn(ov, wout[cols:cols + split, c:c + OUT_COLS])
+    pair_o[1].wait()
+    ov = o_in[:, split:]
+    for c in range(0, d_model, OUT_COLS):
+        out = y_acc[:, c:c + OUT_COLS] + dot_nn(ov, wout[cols + split:, c:c + OUT_COLS])
         y_ref[:, c:c + OUT_COLS] = (out[:rows, :] + out[rows:, :]).astype(BF16)
 
 
@@ -352,11 +372,11 @@
                 pltpu.VMEM((2 * rows, w_out.shape[1]), F32),
                 pltpu.VMEM((SLOTS, keys, 4 * rows), F32),
                 pltpu.VMEM((SLOTS, keys, 4 * rows), BF16),
-                pltpu.SemaphoreType.DMA((14,)),
+                pltpu.SemaphoreType.DMA((13,)),
                 pltpu.SemaphoreType.DMA((1,)),
                 pltpu.SemaphoreType.DMA((3,)),
-                pltpu.SemaphoreType.DMA((3,)),
-                pltpu.SemaphoreType.DMA((3,)),
+                pltpu.SemaphoreType.DMA((4,)),
+                pltpu.SemaphoreType.DMA((4,)),
             ],
             compiler_params=pltpu.CompilerParams(collective_id=0, has_side_effects=True, vmem_limit_bytes=42 * 1024 * 1024),
         )(*operands)

time: 13.9 us -> 13.7 us (0.986)
  Pallas kernels: 13.1 us -> 12.9 us
    pallas_call x1, Pallas kernels: 13.1 us -> 12.9 us  [per_device(): pl.pallas_call(functools.partial(kernel, n, rows, rope, nope), out_shape=...]
where the time goes in v7:
time: 13.7 us; the launch traced here: 13.6 us
  Pallas kernels  12.9 us (94%)
  local copies, waits for them, and re-layouts  0.73 us (5%)
    pallas_call x1, Pallas kernels, per_device(): pl.pallas_call(functools.partial(kernel, n, rows, rope, nope), out_shape=...  12.9 us
    unnamed x1, local copies, waits for them, and re-layouts  0.73 us

profile of v7, /device:TPU:0, one launch (start us, length us, event | category | flops | bytes accessed | tf_op | source)
XLA Modules:
  0.0 13.6 jit_solution(6446874125949197096)
XLA Ops:
  0.0 12.9 %shard_map.118 = bf16[64,2560]{1,0:T(8,128)(2,1)S(1)} custom-call(bf16[64,2560]{1,0:T(8,128)(2,1)} %x_hbm.1, s32[1,64]{1,0:T(1,128)} %bitcast.3, bf16[2560,768]{1,0:T(8,128)(2,1)} %wdq_hbm.1, bf16[768,2560]{1,0:T(8,128)(2,1)} %wuq_hbm.1, bf16[768,1280]{1,0:T(8,128)(2,1)} %wqr_hbm.1, bf16[2560,256]{1,0:T(8,128)(2,1)} %wdkv_hbm.1, bf16[32,2560]{1,0:T(8,128)(2,1)} %bitcast.2, ...), custom_call_target="tpu_custom_call" | custom-call | tf_op jit(solution)/shard_map/pallas_call | solution.py:348
  12.9 0.7 %copy.14 = bf16[64,2560]{1,0:T(8,128)(2,1)} copy(bf16[64,2560]{1,0:T(8,128)(2,1)S(1)} %shard_map.118) | data formatting | bytes 655360

commit v8 on v7

--- a/solution.py
+++ b/solution.py
@@ -17,7 +17,7 @@
 STAGES = ((4, 6, 8), (2, 4, 6))
 LEAD = 2
 SLOTS = 10
-FIRST_SEND = 6
+SENDS = (0, 4, 10)
 OUT_COLS = 512
 STRIP = 32
 
@@ -291,8 +291,9 @@
                 both = [ot[:rows, :], ot[rows:, :]]
                 o_own[0:rows, lanes] = jnp.where(core == 0, both[0], both[1])
                 o_out[:, lanes] = jnp.where(core == 0, both[1], both[0])
-                if g == FIRST_SEND - 1:
-                    pair_o.append(send_heads(0, FIRST_SEND, 2))
+                if g + 1 in SENDS:
+                    last = SENDS.index(g + 1)
+                    pair_o.append(send_heads(SENDS[last - 1], g + 1, 1 + last))
 
         tops, sums, outs = {}, {}, {}
         lags = STAGES[len(owners) - 1]
@@ -311,22 +312,21 @@
     wait_all(gath.at[pl.ds(0, 4)], recv_sem.at[2])
     attend(2)
 
-    pair_o.append(send_heads(FIRST_SEND, groups, 3))
     wait_all(gath.at[pl.ds(0, n - 1)], send_sem.at[0])
     wait_all(wout, load_sem.at[ukv + 1])
     ov = o_own[...]
     for c in range(0, d_model, OUT_COLS):
         y_acc[:, c:c + OUT_COLS] = dot_nn(ov, wout[:cols, c:c + OUT_COLS])
-    split = FIRST_SEND * LANES
-    pair_o[0].wait()
-    ov = o_in[:, :split]
-    for c in range(0, d_model, OUT_COLS):
-        y_acc[:, c:c + OUT_COLS] += dot_nn(ov, wout[cols:cols + split, c:c + OUT_COLS])
-    pair_o[1].wait()
-    ov = o_in[:, split:]
-    for c in range(0, d_model, OUT_COLS):
-        out = y_acc[:, c:c + OUT_COLS] + dot_nn(ov, wout[cols + split:, c:c + OUT_COLS])
-        y_ref[:, c:c + OUT_COLS] = (out[:rows, :] + out[rows:, :]).astype(BF16)
+    for i, copy in enumerate(pair_o):
+        copy.wait()
+        first, last = SENDS[i] * LANES, SENDS[i + 1] * LANES
+        ov = o_in[:, first:last]
+        for c in range(0, d_model, OUT_COLS):
+            out = y_acc[:, c:c + OUT_COLS] + dot_nn(ov, wout[cols + first:cols + last, c:c + OUT_COLS])
+            if last < cols:
+                y_acc[:, c:c + OUT_COLS] = out
+            else:
+                y_ref[:, c:c + OUT_COLS] = (out[:rows, :] + out[rows:, :]).astype(BF16)
 
 
 def solution(mesh):
@@ -375,8 +375,8 @@
                 pltpu.SemaphoreType.DMA((13,)),
                 pltpu.SemaphoreType.DMA((1,)),
                 pltpu.SemaphoreType.DMA((3,)),
-                pltpu.SemaphoreType.DMA((4,)),
-                pltpu.SemaphoreType.DMA((4,)),
+                pltpu.SemaphoreType.DMA((1 + len(SENDS),)),
+                pltpu.SemaphoreType.DMA((1 + len(SENDS),)),
             ],
             compiler_params=pltpu.CompilerParams(collective_id=0, has_side_effects=True, vmem_limit_bytes=42 * 1024 * 1024),
         )(*operands)

time: 13.7 us -> 13.6 us (level)
  Pallas kernels: 12.9 us -> 12.7 us
    pallas_call x1, Pallas kernels: 12.9 us -> 12.7 us  [per_device(): pl.pallas_call(functools.partial(kernel, n, rows, rope, nope), out_shape=...]
where the time goes in v8:
time: 13.6 us; the launch traced here: 13.5 us
  Pallas kernels  12.7 us (93%)
  local copies, waits for them, and re-layouts  0.73 us (5%)
    pallas_call x1, Pallas kernels, per_device(): pl.pallas_call(functools.partial(kernel, n, rows, rope, nope), out_shape=...  12.7 us
    unnamed x1, local copies, waits for them, and re-layouts  0.73 us

profile of v8, /device:TPU:0, one launch (start us, length us, event | category | flops | bytes accessed | tf_op | source)
XLA Modules:
  0.0 13.5 jit_solution(8372831740543925252)
XLA Ops:
  0.0 12.7 %shard_map.118 = bf16[64,2560]{1,0:T(8,128)(2,1)S(1)} custom-call(bf16[64,2560]{1,0:T(8,128)(2,1)} %x_hbm.1, s32[1,64]{1,0:T(1,128)} %bitcast.3, bf16[2560,768]{1,0:T(8,128)(2,1)} %wdq_hbm.1, bf16[768,2560]{1,0:T(8,128)(2,1)} %wuq_hbm.1, bf16[768,1280]{1,0:T(8,128)(2,1)} %wqr_hbm.1, bf16[2560,256]{1,0:T(8,128)(2,1)} %wdkv_hbm.1, bf16[32,2560]{1,0:T(8,128)(2,1)} %bitcast.2, ...), custom_call_target="tpu_custom_call" | custom-call | tf_op jit(solution)/shard_map/pallas_call | solution.py:348
  12.7 0.7 %copy.14 = bf16[64,2560]{1,0:T(8,128)(2,1)} copy(bf16[64,2560]{1,0:T(8,128)(2,1)S(1)} %shard_map.118) | data formatting | bytes 655360

commit v9 on v8

--- a/solution.py
+++ b/solution.py
@@ -166,7 +166,7 @@
 
     send(1, 0, 0)
     for k in range(3):
-        flip_chip = lax.rem(k + 2 * (chip // 3), 3) + 1
+        flip_chip = lax.rem(k + 2 * bit1, 3) + 1
         for flip_core in range(2):
             send(flip_core, flip_chip, (flip_chip + 2) // 2)
 
@@ -245,7 +245,12 @@
 
         def project(c):
             kn_s[0:keys, c:c + 256] = dot_nn(c_all, wukv[0, :, c:c + 256]).astype(BF16)
-            vt_s[c:c + 256, 0:keys] = dot_tt(wukv[1, :, c:c + 256], c_all).astype(BF16)
+            if keys > LANES:
+                vt_s[c:c + 256, 0:keys] = dot_tt(wukv[1, :, c:c + 256], c_all).astype(BF16)
+            else:
+                vals = dot_nn(c_all, wukv[1, :, c:c + 256]).astype(BF16)
+                for t in range(0, 256, LANES):
+                    vt_s[c + t:c + t + LANES, 0:keys] = jnp.transpose(vals[:, t:t + LANES])
 
         def score(g):
             s = dot_nn(jnp.concatenate([kn_s[0:keys, g * LANES:(g + 1) * LANES], krep], axis=1), qbd[g])

time: 13.6 us -> 13.5 us (level)
  no operation moved by 1% of the time
where the time goes in v9:
time: 13.5 us; the launch traced here: 13.4 us
  Pallas kernels  12.7 us (94%)
  local copies, waits for them, and re-layouts  0.73 us (5%)
    pallas_call x1, Pallas kernels, per_device(): pl.pallas_call(functools.partial(kernel, n, rows, rope, nope), out_shape=...  12.7 us
    unnamed x1, local copies, waits for them, and re-layouts  0.73 us

profile of v9, /device:TPU:0, one launch (start us, length us, event | category | flops | bytes accessed | tf_op | source)
XLA Modules:
  0.0 13.4 jit_solution(9156444126805227739)
XLA Ops:
  0.0 12.7 %shard_map.118 = bf16[64,2560]{1,0:T(8,128)(2,1)S(1)} custom-call(bf16[64,2560]{1,0:T(8,128)(2,1)} %x_hbm.1, s32[1,64]{1,0:T(1,128)} %bitcast.3, bf16[2560,768]{1,0:T(8,128)(2,1)} %wdq_hbm.1, bf16[768,2560]{1,0:T(8,128)(2,1)} %wuq_hbm.1, bf16[768,1280]{1,0:T(8,128)(2,1)} %wqr_hbm.1, bf16[2560,256]{1,0:T(8,128)(2,1)} %wdkv_hbm.1, bf16[32,2560]{1,0:T(8,128)(2,1)} %bitcast.2, ...), custom_call_target="tpu_custom_call" | custom-call | tf_op jit(solution)/shard_map/pallas_call | solution.py:353
  12.7 0.7 %copy.14 = bf16[64,2560]{1,0:T(8,128)(2,1)} copy(bf16[64,2560]{1,0:T(8,128)(2,1)S(1)} %shard_map.118) | data formatting | bytes 655360

commit v10 on v9

--- a/solution.py
+++ b/solution.py
@@ -14,7 +14,7 @@
 F32 = jnp.float32
 BF16 = jnp.bfloat16
 LANES = 128
-STAGES = ((4, 6, 8), (2, 4, 6))
+STAGES = ((5, 7, 9), (2, 4, 6))
 LEAD = 2
 SLOTS = 10
 SENDS = (0, 4, 10)

time: 13.5 us -> 13.6 us (level)
  no operation moved by 1% of the time
where the time goes in v10:
time: 13.6 us; the launch traced here: 13.5 us
  Pallas kernels  12.7 us (93%)
  local copies, waits for them, and re-layouts  0.73 us (5%)
    pallas_call x1, Pallas kernels, per_device(): pl.pallas_call(functools.partial(kernel, n, rows, rope, nope), out_shape=...  12.7 us
    unnamed x1, local copies, waits for them, and re-layouts  0.73 us

profile of v10, /device:TPU:0, one launch (start us, length us, event | category | flops | bytes accessed | tf_op | source)
XLA Modules:
  0.0 13.5 jit_solution(16509812727704492398)
XLA Ops:
  0.0 12.7 %shard_map.118 = bf16[64,2560]{1,0:T(8,128)(2,1)S(1)} custom-call(bf16[64,2560]{1,0:T(8,128)(2,1)} %x_hbm.1, s32[1,64]{1,0:T(1,128)} %bitcast.3, bf16[2560,768]{1,0:T(8,128)(2,1)} %wdq_hbm.1, bf16[768,2560]{1,0:T(8,128)(2,1)} %wuq_hbm.1, bf16[768,1280]{1,0:T(8,128)(2,1)} %wqr_hbm.1, bf16[2560,256]{1,0:T(8,128)(2,1)} %wdkv_hbm.1, bf16[32,2560]{1,0:T(8,128)(2,1)} %bitcast.2, ...), custom_call_target="tpu_custom_call" | custom-call | tf_op jit(solution)/shard_map/pallas_call | solution.py:353
  12.7 0.7 %copy.14 = bf16[64,2560]{1,0:T(8,128)(2,1)} copy(bf16[64,2560]{1,0:T(8,128)(2,1)S(1)} %shard_map.118) | data formatting | bytes 655360
